TPU v7x, 512 devices: a whole 4x8x8 slice. The times are simulated.
512 devices in a mesh: row: 64 (over z_lo, y, core), vec: 8 (over z_hi, x).
Axes of the slice: x: 4, y: 8, z: 8 (z_hi: 2, z_lo: 4; z = z_hi * 4 + z_lo), core: 2. Of those that a mesh axis runs over, the one named last changes fastest.
Arguments:
- eigvecs: float32 [32768, 8192], P('row', 'vec'), may hold values from -6 to 6
- reflectors: float32 [6, 32768, 128], P(None, 'row', 'vec'), may hold values from -0.375 to 0.375
- factors: float32 [6, 128, 128, 128], P(None, 'row', 'vec'), may hold values from -0.25 to 0.25
Outputs:
- vectors: float32 [32768, 8192], P('row', 'vec')
All inputs are finite; a program needn't handle non-finite values.
Results may differ from a plain program's by a relative error of at most 0.0001.
Values sent between devices are 32-bit elements; how exact they have to be, the bound alone decides.
No kernel may reach another device: no remote copies, remote signals or barrier semaphores. Data moves between devices by JAX's collectives and lax.ppermute only.
A program may use at most 64 MiB of HBM per device.

v0:
```python
import jax
import jax.numpy as jnp
from jax import lax
from jax.experimental import pallas as pl
from jax.experimental.pallas import tpu as pltpu
from jax.sharding import PartitionSpec as P


NB = 128
F32 = jnp.float32
BF16 = jnp.bfloat16
SPAN = 512
XS = 4
SHIFTED = ((1, 1), (2, 1), (3, 0), (3, 1), (4, 0), (4, 1), (5, 0), (5, 1))


def split(x):
    high = x.astype(BF16)
    return high, (x - high.astype(F32)).astype(BF16)


def mm(a, b):
    return jnp.dot(a, b, preferred_element_type=F32)


def dot3(a, b):
    return mm(a[0], b[0]) + (mm(a[0], b[1]) + mm(a[1], b[0]))


def product(a, b):
    return dot3(split(a), split(b))


def place():
    vec = lax.axis_index("vec")
    return lax.shift_right_logical(vec, 2), vec & 3, lax.axis_index("row") & 1


def assemble(parts, buf, start=0):
    far, near, _ = place()
    width = buf.shape[2]
    for step, part in zip((0, -1, 1, 2), parts):
        x = (near + step) & 3
        for z in range(2):
            buf[(far ^ z) * XS + x] = part[16 * z : 16 * z + 16, start : start + width]


def block(buf, start, width):
    return buf[:, :, start : start + width].reshape(NB, width)


def group_matrix(basis_t, factor):
    return product(basis_t.T, product(factor, basis_t))


def put(refs, index, value):
    high, low = split(value)
    refs[0][index] = high
    refs[1][index] = low


def get(refs, *index):
    return refs[0][index], refs[1][index]


def look_ahead(side, nxt_t, matrix):
    zero = jnp.zeros((NB, NB), F32)
    if side == 0:
        return jnp.concatenate([nxt_t, zero], axis=1) - product(nxt_t, matrix[:NB])
    return jnp.concatenate([zero, nxt_t], axis=1) - product(nxt_t, matrix[NB:])


def spans(body, width):
    def step(c, carry):
        body(pl.ds(pl.multiple_of(c * SPAN, SPAN), SPAN))
        return carry

    lax.fori_loop(0, width // SPAN, step, 0)


def first_payload_kernel(turned, factors, out, shifted, turned_here, factors_here, sem):
    copies = [
        pltpu.make_async_copy(turned, turned_here, sem.at[0]),
        pltpu.make_async_copy(factors, factors_here, sem.at[1]),
    ]
    for copy in copies:
        copy.start()
    for copy in copies:
        copy.wait()
    out[:, 0:512] = turned_here[0]
    out[:, 512:640] = turned_here[1, :, 0:128]
    out[:, 640:768] = turned_here[1, :, 384:512]
    out[:, 768:896] = factors_here[0, 0]
    out[:, 896:1024] = factors_here[0, 1]
    for k, (r, g) in enumerate(SHIFTED):
        shifted[:, k * NB : (k + 1) * NB] = factors_here[r, g]


def rest_payload_kernel(turned, factors, slid, out):
    def came(k):
        return slid[:, k * NB : (k + 1) * NB]

    def middle(r):
        return turned[r, :, 128:384]

    def ends(r):
        return [turned[r, :, 0:128], turned[r, :, 384:512]]

    at = 0
    for part in (
        middle(1), factors[1, 0], factors[1, 1], came(0), turned[2], came(1), factors[2, 0], *ends(3),
        middle(3), came(3), factors[3, 0], came(2), turned[4], came(4), came(5), *ends(5),
        middle(5), came(6), came(7),
    ):
        out[:, at : at + part.shape[1]] = part
        at += part.shape[1]


def first_kernel(own, left, right, across, x, u, chip, core, nxt_t, buf, oph, opl):
    op = (oph, opl)
    assemble((own, left, right, across), buf)
    odd = place()[2] == 1
    for side in range(2):
        nxt = block(buf, 512 + side * NB, NB)
        nxt_t[side] = nxt
        matrix = group_matrix(block(buf, side * 256, 256), block(buf, 768 + side * NB, NB))
        put(op, side, jnp.concatenate([matrix, look_ahead(side, nxt, matrix)], axis=0))

    def body(cols):
        heads = []
        for side in range(2):
            rows = slice(side * 256, side * 256 + 256)
            panel = x[rows, cols]
            image = dot3(get(op, side), split(panel))
            u[rows, cols] = panel - image[:256]
            heads.append(image[256:])
        chip[:, cols] = jnp.where(odd, heads[1], heads[0])
        core[:, cols] = jnp.where(odd, heads[0], heads[1])

    spans(body, x.shape[1])


def middle_kernel(number, own, left, right, across, prev_t, u_in, *rest):
    last = number == 3
    if number == 1:
        u, ph, pl_, uh, ul, qh, ql, ahead, nxt_t, extra, buf, mh, ml, lh, ll, tail = rest
        assemble((own, left, right, across), tail, 3 * 1280 - NB)
        for k in range(8):
            extra[:, k * NB : (k + 1) * NB] = tail[k]
    elif number == 2:
        u, ph, pl_, uh, ul, qh, ql, ahead, nxt_t, buf, mh, ml, lh, ll = rest
    else:
        got_chip, got_core, u, uh, ul, buf, mh, ml = rest
    mid = (mh, ml)
    assemble((own, left, right, across), buf, (number - 1) * 1664)
    at = 0
    put(mid, slice(None), group_matrix(block(buf, at, 256), block(buf, at + 256, NB)))
    spread = []
    for side in range(2):
        if last and side == 0:
            came = jnp.where(place()[2] == 1, got_core[NB:, :], got_chip[NB:, :])
            factor = jnp.concatenate([came[:, k * NB : (k + 1) * NB] for k in range(8)], axis=0)
        else:
            factor = block(buf, at + (512 if side == 0 else 384), NB)
        value = product(prev_t[side].T, factor)
        put((uh, ul), side, value)
        spread.append(value)
    if not last:
        for side in range(2):
            factor = block(buf, at + 1152 + side * NB, NB)
            nxt = block(buf, at + 1408 + side * NB, NB)
            nxt_t[side] = nxt
            matrix = group_matrix(block(buf, at + 640 + side * 256, 256), factor)
            put((ph, pl_), side, matrix)
            look = look_ahead(side, nxt, matrix)
            put((lh, ll), side, look)
            put((qh, ql), side, product(look[:, :NB] if side == 0 else look[:, NB:], spread[side]))

    def body(cols):
        panel = u_in[128:384, cols]
        panel = panel - dot3(get(mid, slice(None)), split(panel))
        u[128:384, cols] = panel
        top, bottom = u_in[0:128, cols], u_in[384:512, cols]
        u[0:128, cols] = top
        u[384:512, cols] = bottom
        if not last:
            ahead[0, :, cols] = dot3(get((lh, ll), 0), split(jnp.concatenate([top, panel[:NB]], axis=0)))
            ahead[1, :, cols] = dot3(get((lh, ll), 1), split(jnp.concatenate([panel[NB:], bottom], axis=0)))

    spans(body, u.shape[1])


def next_kernel(own_chip, got_chip, own_core, got_core, qh, ql, ahead, *rest):
    *extra, chip, core = rest
    odd = place()[2]
    for value in extra:
        chip[NB:, :] = value[...]
        core[NB:, :] = value[...]

    def body(cols):
        for own, got, out, side in ((own_chip, got_chip, chip, odd), (own_core, got_core, core, 1 - odd)):
            total = own[:NB, cols] + got[:NB, cols]
            out[:NB, cols] = ahead[side, :, cols] - dot3((qh[side], ql[side]), split(total))

    spans(body, chip.shape[1])


def even_kernel(last, own_chip, got_chip, own_core, got_core, uh, ul, *rest):
    if last:
        u_in, u = rest
    else:
        ph, pl_, u_in, u = rest
    odd = place()[2] == 1

    def body(cols):
        chip = own_chip[:NB, cols] + got_chip[:NB, cols]
        core = own_core[:NB, cols] + got_core[:NB, cols]
        totals = (jnp.where(odd, core, chip), jnp.where(odd, chip, core))
        for side in range(2):
            near = slice(0, 128) if side == 0 else slice(384, 512)
            far = slice(128, 256) if side == 0 else slice(256, 384)
            panel = u_in[near, cols] - dot3((uh[side], ul[side]), split(totals[side]))
            if last:
                u[near, cols] = panel
                u[far, cols] = u_in[far, cols]
            else:
                rows = slice(side * 256, side * 256 + 256)
                pair = [panel, u_in[far, cols]] if side == 0 else [u_in[far, cols], panel]
                both = jnp.concatenate(pair, axis=0)
                u[rows, cols] = both - dot3((ph[side], pl_[side]), split(both))

    spans(body, u.shape[1])


def call(kernel, outs, scratch, flops, *args, far=(), sems=0):
    vmem = pl.BlockSpec(memory_space=pltpu.VMEM)
    hbm = pl.BlockSpec(memory_space=pltpu.HBM)
    return pl.pallas_call(
        kernel,
        out_shape=[jax.ShapeDtypeStruct(s, t) for s, t in outs],
        in_specs=[hbm if k in far else vmem for k in range(len(args))],
        out_specs=[vmem] * len(outs),
        scratch_shapes=[pltpu.VMEM(s, t) for s, t in scratch] + [pltpu.SemaphoreType.DMA((sems,))] * bool(sems),
        cost_estimate=pl.CostEstimate(flops=flops, bytes_accessed=4 << 20, transcendentals=0),
        compiler_params=pltpu.CompilerParams(vmem_limit_bytes=24 << 20),
    )(*args)


def far_half(payload):
    return lax.ppermute(payload, "vec", [(v, v ^ XS) for v in range(2 * XS)])


def near_parts(payload, other):
    both = jnp.concatenate([payload, other], axis=0)
    parts = [
        lax.ppermute(both, "vec", [(v, (v & XS) + ((v + step) & 3)) for v in range(2 * XS)])
        for step in (1, -1, 2)
    ]
    return (both, *parts)


def rounds(eigvecs, reflectors, factors):
    rows = lax.axis_size("row")
    chip_pairs = [p for k in range(1, rows - 1, 2) for p in ((k, k + 1), (k + 1, k))]
    core_pairs = [(k, k ^ 1) for k in range(rows)]
    turned = jnp.transpose(reflectors, (0, 2, 1))
    a, shifted, turned, factors = call(
        first_payload_kernel,
        [((16, 1024), F32), ((16, 1024), F32), (turned.shape, F32), (factors.shape, F32)],
        [],
        1 << 20,
        turned,
        factors,
        far=(0, 1),
        sems=2,
    )
    slid = lax.ppermute(shifted, "row", [(k, k + 1) for k in range(rows - 1)])
    a2 = far_half(a)
    (b,) = call(rest_payload_kernel, [((16, 3840), F32)], [], 1 << 20, turned, factors, slid)
    b2 = far_half(b)
    a = near_parts(a, a2)
    b = near_parts(b, b2)

    width = eigvecs.shape[1]
    whole = ((4 * NB, width), F32)
    strip = ((NB, width), F32)
    pair = ((2, 2 * NB, 2 * NB), BF16)
    small = ((2, NB, NB), BF16)
    ends = ((2, NB, NB), F32)
    strips = ((2, NB, width), F32)
    look = ((2, NB, 2 * NB), BF16)
    mid = ((2 * NB, 2 * NB), BF16)
    op = ((2, 3 * NB, 2 * NB), BF16)

    def held(lanes):
        return ((2 * XS, 16, lanes), F32)

    def swap(chip, core):
        return lax.ppermute(chip, "row", chip_pairs), lax.ppermute(core, "row", core_pairs)

    unit = 2 * NB * NB * width * 3
    u, chip, core, nxt_t = call(first_kernel, [whole, strip, strip, ends], [held(1024), op, op], 12 * unit, *a, eigvecs)
    longer = ((NB + 16, width), F32)
    for number in (1, 2):
        got_chip, got_core = swap(chip, core)
        u, ph, pl_, uh, ul, qh, ql, ahead, nxt_t, *extra = call(
            lambda *refs, number=number: middle_kernel(number, *refs),
            [whole, pair, pair, small, small, small, small, strips, ends] + [((16, width), F32)] * (2 - number),
            [held(1664), mid, mid, look, look] + [held(NB)] * (2 - number),
            10 * unit,
            *b, nxt_t, u,
        )
        sent = longer if number == 1 else strip
        new_chip, new_core = call(
            next_kernel,
            [sent, sent],
            [],
            2 * unit,
            chip, got_chip, core, got_core, qh, ql, ahead, *extra,
        )
        (u,) = call(
            lambda *refs: even_kernel(False, *refs),
            [whole],
            [],
            10 * unit,
            chip, got_chip, core, got_core, uh, ul, ph, pl_, u,
        )
        if number == 2:
            came_chip, came_core = got_chip, got_core
        chip, core = new_chip, new_core
    got_chip, got_core = swap(chip, core)
    u, uh, ul = call(
        lambda *refs: middle_kernel(3, *refs),
        [whole, small, small],
        [held(512), mid, mid],
        5 * unit,
        *b, nxt_t, u, came_chip, came_core,
    )
    (u,) = call(
        lambda *refs: even_kernel(True, *refs),
        [whole],
        [],
        2 * unit,
        chip, got_chip, core, got_core, uh, ul, u,
    )
    return u


def solution(mesh):
    return jax.shard_map(
        rounds,
        mesh=mesh,
        in_specs=(P("row", "vec"), P(None, "row", "vec"), P(None, "row", "vec", None)),
        out_specs=P("row", "vec"),
        check_vma=False,
    )
```

profile of v0, /device:TPU:64, one launch (start us, length us, event | category | flops | bytes accessed | tf_op | source)
XLA Modules:
  0.0 102.0 jit_solution(10843462024052420722)
XLA Ops:
  0.0 0.0 copy-start
  0.0 0.9 copy-done
  0.9 0.0 copy-start.1
  0.9 0.9 copy-done.1
  1.8 0.0 copy-start.2
  1.8 0.4 shard_map.37
  2.2 2.1 %collective-permute-start.6 = (f32[16,1024]{1,0:T(8,128)S(1)}, f32[16,1024]{1,0:T(8,128)S(1)}, u32[]{:S(2)}, u32[]{:S(2)}) collective-permute-start(f32[16,1024]{1,0:T(8,128)S(1)} %get-tuple-element.44), channel_id=1, source_target_pairs={{0,8},{8,16},{16,24},{24,32},{32,40},{40,48},{48,56},{56,64},{64,7... | collective-permute-start | bytes 196616 | tf_op jit(solution)/shard_map/ppermute | solution.py:277
  4.3 5.8 %collective-permute-done.6.slid = f32[16,1024]{1,0:T(8,128)S(1)} collective-permute-done((f32[16,1024]{1,0:T(8,128)S(1)}, f32[16,1024]{1,0:T(8,128)S(1)}, u32[]{:S(2)}, u32[]{:S(2)}) %collective-permute-start.6) | collective-permute-done | bytes 65568 | tf_op jit(solution)/shard_map/ppermute | solution.py:277
  10.1 10.0 %collective-permute-start.7 = (f32[16,3840]{1,0:T(8,128)S(1)}, f32[16,3840]{1,0:T(8,128)S(1)}, u32[]{:S(2)}, u32[]{:S(2)}) collective-permute-start(f32[16,3840]{1,0:T(8,128)S(1)} %shard_map.39), channel_id=1, source_target_pairs={{0,4},{1,5},{2,6},{3,7},{4,0},{5,1},{6,2},{7,3},{8,12},{9,13},{10,... | collective-permute-start | bytes 737288 | tf_op jit(solution)/shard_map/ppermute | solution.py:250
  20.1 1.9 %collective-permute-start = (f32[16,1024]{1,0:T(8,128)S(1)}, f32[16,1024]{1,0:T(8,128)S(1)}, u32[]{:S(2)}, u32[]{:S(2)}) collective-permute-start(f32[16,1024]{1,0:T(8,128)S(1)} %get-tuple-element.39), channel_id=1, source_target_pairs={{0,4},{1,5},{2,6},{3,7},{4,0},{5,1},{6,2},{7,3},{8,12},{9,13},{10,... | collective-permute-start | bytes 196616 | tf_op jit(solution)/shard_map/ppermute | solution.py:250
  22.0 8.2 %collective-permute-done = f32[16,1024]{1,0:T(8,128)S(1)} collective-permute-done((f32[16,1024]{1,0:T(8,128)S(1)}, f32[16,1024]{1,0:T(8,128)S(1)}, u32[]{:S(2)}, u32[]{:S(2)}) %collective-permute-start) | collective-permute-done | bytes 65568 | tf_op jit(solution)/shard_map/ppermute | solution.py:250
  30.3 5.0 %collective-permute-start.3 = (f32[32,1024]{1,0:T(8,128)S(1)}, f32[32,1024]{1,0:T(8,128)S(1)}, u32[]{:S(2)}, u32[]{:S(2)}) collective-permute-start(f32[32,1024]{1,0:T(8,128)S(1)} %constant_dynamic-update-slice_fusion.own), channel_id=1, source_target_pairs={{0,2},{1,3},{2,0},{3,1},{4,6},{5,7},{6,4},{7,5},{8,10},{9,11},{10,... | collective-permute-start | bytes 393224 | tf_op jit(solution)/shard_map/ppermute | solution.py:256
  35.2 3.0 %collective-permute-start.2 = (f32[32,1024]{1,0:T(8,128)S(1)}, f32[32,1024]{1,0:T(8,128)S(1)}, u32[]{:S(2)}, u32[]{:S(2)}) collective-permute-start(f32[32,1024]{1,0:T(8,128)S(1)} %constant_dynamic-update-slice_fusion.own), channel_id=1, source_target_pairs={{0,3},{1,0},{2,1},{3,2},{4,7},{5,4},{6,5},{7,6},{8,11},{9,8},{10,9... | collective-permute-start | bytes 393224 | tf_op jit(solution)/shard_map/ppermute | solution.py:256
  38.3 2.8 %collective-permute-start.1 = (f32[32,1024]{1,0:T(8,128)S(1)}, f32[32,1024]{1,0:T(8,128)S(1)}, u32[]{:S(2)}, u32[]{:S(2)}) collective-permute-start(f32[32,1024]{1,0:T(8,128)S(1)} %constant_dynamic-update-slice_fusion.own), channel_id=1, source_target_pairs={{0,1},{1,2},{2,3},{3,0},{4,5},{5,6},{6,7},{7,4},{8,9},{9,10},{10,1... | collective-permute-start | bytes 393224 | tf_op jit(solution)/shard_map/ppermute | solution.py:256
  41.1 0.0 collective-permute-done.7
  41.1 2.6 %collective-permute-start.10 = (f32[32,3840]{1,0:T(8,128)S(1)}, f32[32,3840]{1,0:T(8,128)S(1)}, u32[]{:S(2)}, u32[]{:S(2)}) collective-permute-start(f32[32,3840]{1,0:T(8,128)S(1)} %pad_maximum_fusion.refs_0_), channel_id=1, source_target_pairs={{0,2},{1,3},{2,0},{3,1},{4,6},{5,7},{6,4},{7,5},{8,10},{9,11},{10,... | collective-permute-start | bytes 1474568 | tf_op jit(solution)/shard_map/ppermute | solution.py:256
  43.7 4.5 %collective-permute-start.9 = (f32[32,3840]{1,0:T(8,128)S(1)}, f32[32,3840]{1,0:T(8,128)S(1)}, u32[]{:S(2)}, u32[]{:S(2)}) collective-permute-start(f32[32,3840]{1,0:T(8,128)S(1)} %pad_maximum_fusion.refs_0_), channel_id=1, source_target_pairs={{0,3},{1,0},{2,1},{3,2},{4,7},{5,4},{6,5},{7,6},{8,11},{9,8},{10,9... | collective-permute-start | bytes 1474568 | tf_op jit(solution)/shard_map/ppermute | solution.py:256
  48.2 0.0 collective-permute-done.3.across
  48.3 1.9 %collective-permute-start.8 = (f32[32,3840]{1,0:T(8,128)S(1)}, f32[32,3840]{1,0:T(8,128)S(1)}, u32[]{:S(2)}, u32[]{:S(2)}) collective-permute-start(f32[32,3840]{1,0:T(8,128)S(1)} %pad_maximum_fusion.refs_0_), channel_id=1, source_target_pairs={{0,1},{1,2},{2,3},{3,0},{4,5},{5,6},{6,7},{7,4},{8,9},{9,10},{10,1... | collective-permute-start | bytes 1474568 | tf_op jit(solution)/shard_map/ppermute | solution.py:256
  50.2 0.0 collective-permute-done.2.right
  50.2 6.6 %collective-permute-done.1.left = f32[32,1024]{1,0:T(8,128)S(1)} collective-permute-done((f32[32,1024]{1,0:T(8,128)S(1)}, f32[32,1024]{1,0:T(8,128)S(1)}, u32[]{:S(2)}, u32[]{:S(2)}) %collective-permute-start.1) | collective-permute-done | bytes 131104 | tf_op jit(solution)/shard_map/ppermute | solution.py:256
  56.8 0.0 copy-done.2
  56.8 3.0 %shard_map.38 = (f32[512,1024]{1,0:T(8,128)S(1)}, f32[128,1024]{1,0:T(8,128)S(1)}, f32[128,1024]{1,0:T(8,128)S(1)}, f32[2,128,128]{2,1,0:T(8,128)S(1)}) custom-call(f32[32,1024]{1,0:T(8,128)S(1)} %constant_dynamic-update-slice_fusion.own, f32[32,1024]{1,0:T(8,128)S(1)} %collective-permute-done.1.left, f32[32,1024]{1,0:T(8,128)S(1)} %collective-permute-done.2.right, ...), custom_call_target="tpu_custom_call" | custom-call | flops 1207959552 | bytes 4194304 | tf_op jit(solution)/shard_map/pallas_call | solution.py:238
  59.9 1.9 %collective-permute-start.4 = (f32[128,1024]{1,0:T(8,128)S(1)}, f32[128,1024]{1,0:T(8,128)S(1)}, u32[]{:S(2)}, u32[]{:S(2)}) collective-permute-start(f32[128,1024]{1,0:T(8,128)S(1)} %get-tuple-element.40.own_chip.refs_0_), channel_id=1, source_target_pairs={{8,16},{16,8},{24,32},{32,24},{40,48},{48,40},{56,64},{64,56},{72,... | collective-permute-start | bytes 1572872 | tf_op jit(solution)/shard_map/ppermute | solution.py:299
  61.8 5.0 %collective-permute-start.5 = (f32[128,1024]{1,0:T(8,128)S(1)}, f32[128,1024]{1,0:T(8,128)S(1)}, u32[]{:S(2)}, u32[]{:S(2)}) collective-permute-start(f32[128,1024]{1,0:T(8,128)S(1)} %get-tuple-element.41.own_core.refs_2_), channel_id=1, source_target_pairs={{0,8},{8,0},{16,24},{24,16},{32,40},{40,32},{48,56},{56,48},{64,72... | collective-permute-start | bytes 1572872 | tf_op jit(solution)/shard_map/ppermute | solution.py:299
  66.8 0.0 collective-permute-done.10.refs_3_
  66.8 0.0 collective-permute-done.9.refs_2_
  66.8 0.6 collective-permute-done.8.refs_1_
  67.4 3.3 %shard_map.40 = (f32[512,1024]{1,0:T(8,128)S(1)}, bf16[2,256,256]{2,1,0:T(8,128)(2,1)S(1)}, bf16[2,256,256]{2,1,0:T(8,128)(2,1)S(1)}, bf16[2,128,128]{2,1,0:T(8,...) custom-call(f32[32,3840]{1,0:T(8,128)S(1)} %pad_maximum_fusion.refs_, ...), custom_call_target="tpu_custom_call" | custom-call | flops 1006632960 | bytes 4194304 | tf_op jit(solution)/shard_map/pallas_call | solution.py:238
  70.7 1.8 %collective-permute-done.4.got_chip.refs_1_ = f32[128,1024]{1,0:T(8,128)S(1)} collective-permute-done((f32[128,1024]{1,0:T(8,128)S(1)}, f32[128,1024]{1,0:T(8,128)S(1)}, u32[]{:S(2)}, u32[]{:S(2)}) %collective-permute-start.4) | collective-permute-done | bytes 524320 | tf_op jit(solution)/shard_map/ppermute | solution.py:299
  72.5 0.0 collective-permute-done.5.got_core.refs_3_
  72.5 0.7 shard_map.41
  73.2 1.9 %collective-permute-start.11 = (f32[144,1024]{1,0:T(8,128)S(1)}, f32[144,1024]{1,0:T(8,128)S(1)}, u32[]{:S(2)}, u32[]{:S(2)}) collective-permute-start(f32[144,1024]{1,0:T(8,128)S(1)} %get-tuple-element.51.own_chip.refs_0_), channel_id=1, source_target_pairs={{8,16},{16,8},{24,32},{32,24},{40,48},{48,40},{56,64},{64,56},{72,... | collective-permute-start | bytes 1769480 | tf_op jit(solution)/shard_map/ppermute | solution.py:299
  75.2 2.9 %collective-permute-start.12 = (f32[144,1024]{1,0:T(8,128)S(1)}, f32[144,1024]{1,0:T(8,128)S(1)}, u32[]{:S(2)}, u32[]{:S(2)}) collective-permute-start(f32[144,1024]{1,0:T(8,128)S(1)} %get-tuple-element.52.own_core.refs_2_), channel_id=1, source_target_pairs={{0,8},{8,0},{16,24},{24,16},{32,40},{40,32},{48,56},{56,48},{64,72... | collective-permute-start | bytes 1769480 | tf_op jit(solution)/shard_map/ppermute | solution.py:299
  78.0 2.3 %shard_map.42.refs_5_ = f32[512,1024]{1,0:T(8,128)S(1)} custom-call(f32[128,1024]{1,0:T(8,128)S(1)} %get-tuple-element.40.own_chip.refs_0_, f32[128,1024]{1,0:T(8,128)S(1)} %collective-permute-done.4.got_chip.refs_1_, f32[128,1024]{1,0:T(8,128)S(1)} %get-tuple-element.41.own_core.refs_2_, f32[128,1024]{1,0:T(8,128)S(1)} %collective-permute-done.5.got_core.refs_3_, ...), custom_call_target="tpu_custom_call" | custom-call | flops 1006632960 | bytes 4194304 | tf_op jit(solution)/shard_map/pallas_call | solution.py:238
  80.3 3.3 %shard_map.43 = (f32[512,1024]{1,0:T(8,128)S(1)}, bf16[2,256,256]{2,1,0:T(8,128)(2,1)S(1)}, bf16[2,256,256]{2,1,0:T(8,128)(2,1)S(1)}, bf16[2,128,128]{2,1,0:T(8,...) custom-call(f32[32,3840]{1,0:T(8,128)S(1)} %pad_maximum_fusion.refs_, ...), custom_call_target="tpu_custom_call" | custom-call | flops 1006632960 | bytes 4194304 | tf_op jit(solution)/shard_map/pallas_call | solution.py:238
  83.6 3.0 %collective-permute-done.11.got_chip.refs_1_.refs_6_ = f32[144,1024]{1,0:T(8,128)S(1)} collective-permute-done((f32[144,1024]{1,0:T(8,128)S(1)}, f32[144,1024]{1,0:T(8,128)S(1)}, u32[]{:S(2)}, u32[]{:S(2)}) %collective-permute-start.11) | collective-permute-done | bytes 589856 | tf_op jit(solution)/shard_map/ppermute | solution.py:299
  86.5 0.0 collective-permute-done.12.got_core.refs_3_.refs_7_
  86.6 0.7 shard_map.44
  87.3 1.9 %collective-permute-start.13 = (f32[128,1024]{1,0:T(8,128)S(1)}, f32[128,1024]{1,0:T(8,128)S(1)}, u32[]{:S(2)}, u32[]{:S(2)}) collective-permute-start(f32[128,1024]{1,0:T(8,128)S(1)} %get-tuple-element.62.refs_0_), channel_id=1, source_target_pairs={{8,16},{16,8},{24,32},{32,24},{40,48},{48,40},{56,64},{64,56},{72,... | collective-permute-start | bytes 1572872 | tf_op jit(solution)/shard_map/ppermute | solution.py:299
  89.2 1.9 %collective-permute-start.14 = (f32[128,1024]{1,0:T(8,128)S(1)}, f32[128,1024]{1,0:T(8,128)S(1)}, u32[]{:S(2)}, u32[]{:S(2)}) collective-permute-start(f32[128,1024]{1,0:T(8,128)S(1)} %get-tuple-element.63.refs_2_), channel_id=1, source_target_pairs={{0,8},{8,0},{16,24},{24,16},{32,40},{40,32},{48,56},{56,48},{64,72... | collective-permute-start | bytes 1572872 | tf_op jit(solution)/shard_map/ppermute | solution.py:299
  91.2 2.2 %shard_map.45.refs_5_ = f32[512,1024]{1,0:T(8,128)S(1)} custom-call(f32[144,1024]{1,0:T(8,128)S(1)} %get-tuple-element.51.own_chip.refs_0_, f32[144,1024]{1,0:T(8,128)S(1)} %collective-permute-done.11.got_chip.refs_1_.refs_6_, f32[144,1024]{1,0:T(8,128)S(1)} %get-tuple-element.52.own_core.refs_2_, ...), custom_call_target="tpu_custom_call" | custom-call | flops 1006632960 | bytes 4194304 | tf_op jit(solution)/shard_map/pallas_call | solution.py:238
  93.4 1.4 %shard_map.46 = (f32[512,1024]{1,0:T(8,128)S(1)}, bf16[2,128,128]{2,1,0:T(8,128)(2,1)S(1)}, bf16[2,128,128]{2,1,0:T(8,128)(2,1)S(1)}) custom-call(f32[32,3840]{1,0:T(8,128)S(1)} %pad_maximum_fusion.refs_0_, f32[32,3840]{1,0:T(8,128)S(1)} %collective-permute-done.8.refs_1_, f32[32,3840]{1,0:T(8,128)S(1)} %collective-permute-done.9.refs_2_, ...), custom_call_target="tpu_custom_call" | custom-call | flops 503316480 | bytes 4194304 | tf_op jit(solution)/shard_map/pallas_call | solution.py:238
  94.8 5.1 %collective-permute-done.13.refs_1_ = f32[128,1024]{1,0:T(8,128)S(1)} collective-permute-done((f32[128,1024]{1,0:T(8,128)S(1)}, f32[128,1024]{1,0:T(8,128)S(1)}, u32[]{:S(2)}, u32[]{:S(2)}) %collective-permute-start.13) | collective-permute-done | bytes 524320 | tf_op jit(solution)/shard_map/ppermute | solution.py:299
  99.9 0.0 collective-permute-done.14.refs_3_
  99.9 2.1 %shard_map.47 = f32[512,1024]{1,0:T(8,128)} custom-call(f32[128,1024]{1,0:T(8,128)S(1)} %get-tuple-element.62.refs_0_, f32[128,1024]{1,0:T(8,128)S(1)} %collective-permute-done.13.refs_1_, f32[128,1024]{1,0:T(8,128)S(1)} %get-tuple-element.63.refs_2_, f32[128,1024]{1,0:T(8,128)S(1)} %collective-permute-done.14.refs_3_, ...), custom_call_target="tpu_custom_call" | custom-call | flops 201326592 | bytes 4194304 | tf_op jit(solution)/shard_map/pallas_call | solution.py:238
  (4 shorter events, 0.1 us)
Async XLA Ops:
  0.0 0.9 copy-start
  0.9 0.9 copy-start.1
  1.8 55.0 %copy-start.2 = (f32[512,1024]{1,0:T(8,128)S(1)}, f32[512,1024]{1,0:T(8,128)}, u32[]{:S(2)}) copy-start(f32[512,1024]{1,0:T(8,128)} %x.1) | copy-start | bytes 6291460
  2.2 7.8 %collective-permute-start.6 = (f32[16,1024]{1,0:T(8,128)S(1)}, f32[16,1024]{1,0:T(8,128)S(1)}, u32[]{:S(2)}, u32[]{:S(2)}) collective-permute-start(f32[16,1024]{1,0:T(8,128)S(1)} %get-tuple-element.44), channel_id=1, source_target_pairs={{0,8},{8,16},{16,24},{24,32},{32,40},{40,48},{48,56},{56,64},{64,7... | collective-permute-start | bytes 196616 | tf_op jit(solution)/shard_map/ppermute | solution.py:277
  10.1 31.0 %collective-permute-start.7 = (f32[16,3840]{1,0:T(8,128)S(1)}, f32[16,3840]{1,0:T(8,128)S(1)}, u32[]{:S(2)}, u32[]{:S(2)}) collective-permute-start(f32[16,3840]{1,0:T(8,128)S(1)} %shard_map.39), channel_id=1, source_target_pairs={{0,4},{1,5},{2,6},{3,7},{4,0},{5,1},{6,2},{7,3},{8,12},{9,13},{10,... | collective-permute-start | bytes 737288 | tf_op jit(solution)/shard_map/ppermute | solution.py:250
  20.1 10.2 %collective-permute-start = (f32[16,1024]{1,0:T(8,128)S(1)}, f32[16,1024]{1,0:T(8,128)S(1)}, u32[]{:S(2)}, u32[]{:S(2)}) collective-permute-start(f32[16,1024]{1,0:T(8,128)S(1)} %get-tuple-element.39), channel_id=1, source_target_pairs={{0,4},{1,5},{2,6},{3,7},{4,0},{5,1},{6,2},{7,3},{8,12},{9,13},{10,... | collective-permute-start | bytes 196616 | tf_op jit(solution)/shard_map/ppermute | solution.py:250
  30.3 18.0 %collective-permute-start.3 = (f32[32,1024]{1,0:T(8,128)S(1)}, f32[32,1024]{1,0:T(8,128)S(1)}, u32[]{:S(2)}, u32[]{:S(2)}) collective-permute-start(f32[32,1024]{1,0:T(8,128)S(1)} %constant_dynamic-update-slice_fusion.own), channel_id=1, source_target_pairs={{0,2},{1,3},{2,0},{3,1},{4,6},{5,7},{6,4},{7,5},{8,10},{9,11},{10,... | collective-permute-start | bytes 393224 | tf_op jit(solution)/shard_map/ppermute | solution.py:256
  35.2 14.9 %collective-permute-start.2 = (f32[32,1024]{1,0:T(8,128)S(1)}, f32[32,1024]{1,0:T(8,128)S(1)}, u32[]{:S(2)}, u32[]{:S(2)}) collective-permute-start(f32[32,1024]{1,0:T(8,128)S(1)} %constant_dynamic-update-slice_fusion.own), channel_id=1, source_target_pairs={{0,3},{1,0},{2,1},{3,2},{4,7},{5,4},{6,5},{7,6},{8,11},{9,8},{10,9... | collective-permute-start | bytes 393224 | tf_op jit(solution)/shard_map/ppermute | solution.py:256
  38.3 18.5 %collective-permute-start.1 = (f32[32,1024]{1,0:T(8,128)S(1)}, f32[32,1024]{1,0:T(8,128)S(1)}, u32[]{:S(2)}, u32[]{:S(2)}) collective-permute-start(f32[32,1024]{1,0:T(8,128)S(1)} %constant_dynamic-update-slice_fusion.own), channel_id=1, source_target_pairs={{0,1},{1,2},{2,3},{3,0},{4,5},{5,6},{6,7},{7,4},{8,9},{9,10},{10,1... | collective-permute-start | bytes 393224 | tf_op jit(solution)/shard_map/ppermute | solution.py:256
  41.1 25.6 %collective-permute-start.10 = (f32[32,3840]{1,0:T(8,128)S(1)}, f32[32,3840]{1,0:T(8,128)S(1)}, u32[]{:S(2)}, u32[]{:S(2)}) collective-permute-start(f32[32,3840]{1,0:T(8,128)S(1)} %pad_maximum_fusion.refs_0_), channel_id=1, source_target_pairs={{0,2},{1,3},{2,0},{3,1},{4,6},{5,7},{6,4},{7,5},{8,10},{9,11},{10,... | collective-permute-start | bytes 1474568 | tf_op jit(solution)/shard_map/ppermute | solution.py:256
  43.7 23.1 %collective-permute-start.9 = (f32[32,3840]{1,0:T(8,128)S(1)}, f32[32,3840]{1,0:T(8,128)S(1)}, u32[]{:S(2)}, u32[]{:S(2)}) collective-permute-start(f32[32,3840]{1,0:T(8,128)S(1)} %pad_maximum_fusion.refs_0_), channel_id=1, source_target_pairs={{0,3},{1,0},{2,1},{3,2},{4,7},{5,4},{6,5},{7,6},{8,11},{9,8},{10,9... | collective-permute-start | bytes 1474568 | tf_op jit(solution)/shard_map/ppermute | solution.py:256
  48.3 19.2 %collective-permute-start.8 = (f32[32,3840]{1,0:T(8,128)S(1)}, f32[32,3840]{1,0:T(8,128)S(1)}, u32[]{:S(2)}, u32[]{:S(2)}) collective-permute-start(f32[32,3840]{1,0:T(8,128)S(1)} %pad_maximum_fusion.refs_0_), channel_id=1, source_target_pairs={{0,1},{1,2},{2,3},{3,0},{4,5},{5,6},{6,7},{7,4},{8,9},{9,10},{10,1... | collective-permute-start | bytes 1474568 | tf_op jit(solution)/shard_map/ppermute | solution.py:256
  59.9 12.6 %collective-permute-start.4 = (f32[128,1024]{1,0:T(8,128)S(1)}, f32[128,1024]{1,0:T(8,128)S(1)}, u32[]{:S(2)}, u32[]{:S(2)}) collective-permute-start(f32[128,1024]{1,0:T(8,128)S(1)} %get-tuple-element.40.own_chip.refs_0_), channel_id=1, source_target_pairs={{8,16},{16,8},{24,32},{32,24},{40,48},{48,40},{56,64},{64,56},{72,... | collective-permute-start | bytes 1572872 | tf_op jit(solution)/shard_map/ppermute | solution.py:299
  61.8 10.7 %collective-permute-start.5 = (f32[128,1024]{1,0:T(8,128)S(1)}, f32[128,1024]{1,0:T(8,128)S(1)}, u32[]{:S(2)}, u32[]{:S(2)}) collective-permute-start(f32[128,1024]{1,0:T(8,128)S(1)} %get-tuple-element.41.own_core.refs_2_), channel_id=1, source_target_pairs={{0,8},{8,0},{16,24},{24,16},{32,40},{40,32},{48,56},{56,48},{64,72... | collective-permute-start | bytes 1572872 | tf_op jit(solution)/shard_map/ppermute | solution.py:299
  73.2 13.3 %collective-permute-start.11 = (f32[144,1024]{1,0:T(8,128)S(1)}, f32[144,1024]{1,0:T(8,128)S(1)}, u32[]{:S(2)}, u32[]{:S(2)}) collective-permute-start(f32[144,1024]{1,0:T(8,128)S(1)} %get-tuple-element.51.own_chip.refs_0_), channel_id=1, source_target_pairs={{8,16},{16,8},{24,32},{32,24},{40,48},{48,40},{56,64},{64,56},{72,... | collective-permute-start | bytes 1769480 | tf_op jit(solution)/shard_map/ppermute | solution.py:299
  75.2 11.4 %collective-permute-start.12 = (f32[144,1024]{1,0:T(8,128)S(1)}, f32[144,1024]{1,0:T(8,128)S(1)}, u32[]{:S(2)}, u32[]{:S(2)}) collective-permute-start(f32[144,1024]{1,0:T(8,128)S(1)} %get-tuple-element.52.own_core.refs_2_), channel_id=1, source_target_pairs={{0,8},{8,0},{16,24},{24,16},{32,40},{40,32},{48,56},{56,48},{64,72... | collective-permute-start | bytes 1769480 | tf_op jit(solution)/shard_map/ppermute | solution.py:299
  87.3 12.6 %collective-permute-start.13 = (f32[128,1024]{1,0:T(8,128)S(1)}, f32[128,1024]{1,0:T(8,128)S(1)}, u32[]{:S(2)}, u32[]{:S(2)}) collective-permute-start(f32[128,1024]{1,0:T(8,128)S(1)} %get-tuple-element.62.refs_0_), channel_id=1, source_target_pairs={{8,16},{16,8},{24,32},{32,24},{40,48},{48,40},{56,64},{64,56},{72,... | collective-permute-start | bytes 1572872 | tf_op jit(solution)/shard_map/ppermute | solution.py:299
  89.2 10.7 %collective-permute-start.14 = (f32[128,1024]{1,0:T(8,128)S(1)}, f32[128,1024]{1,0:T(8,128)S(1)}, u32[]{:S(2)}, u32[]{:S(2)}) collective-permute-start(f32[128,1024]{1,0:T(8,128)S(1)} %get-tuple-element.63.refs_2_), channel_id=1, source_target_pairs={{0,8},{8,0},{16,24},{24,16},{32,40},{40,32},{48,56},{56,48},{64,72... | collective-permute-start | bytes 1572872 | tf_op jit(solution)/shard_map/ppermute | solution.py:299
where the time goes:
time: 103 us; the launch traced here: 102 us
  starting transfers between devices  49.3 us (48%)
  waiting for transfers between devices  31.1 us (30%)
  Pallas kernels  19.5 us (19%)
  local copies, waits for them, and re-layouts  1.83 us (2%)
    ppermute x6, starting transfers between devices, near_parts(): lax.ppermute(both, 'vec', [(v, (v & XS) + (v + step & 3)) for v in range(...  19.8 us
    pallas_call x11, Pallas kernels, call(): pl.pallas_call(kernel, out_shape=[jax.ShapeDtypeStruct(s, t) for s, t in...  19.5 us
    ppermute x2, starting transfers between devices, far_half(): return lax.ppermute(payload, 'vec', [(v, v ^ XS) for v in range(2 * XS)])  11.9 us
    ppermute x3, waiting for transfers between devices, swap(): lax.ppermute(chip, 'row', chip_pairs)  9.86 us
    ppermute x3, starting transfers between devices, swap(): lax.ppermute(core, 'row', core_pairs)  9.76 us
    ppermute x2, waiting for transfers between devices, far_half(): return lax.ppermute(payload, 'vec', [(v, v ^ XS) for v in range(2 * XS)])  8.23 us
    ppermute x6, waiting for transfers between devices, near_parts(): lax.ppermute(both, 'vec', [(v, (v & XS) + (v + step & 3)) for v in range(...  7.27 us
    ppermute x1, waiting for transfers between devices, rounds(): slid = lax.ppermute(shifted, 'row', [(k, k + 1) for k in range(rows - 1)])  5.77 us
  transfers between devices with their start and end apart: 15, of which 7 were waited for; matrix products, arithmetic and copies ran while one was open for 0% of the time, Pallas kernels for 15%

commit v1 on v0

v1 whole, which is shorter than its diff:
```python
import jax
import jax.numpy as jnp
from jax import lax
from jax.experimental import pallas as pl
from jax.experimental.pallas import tpu as pltpu
from jax.sharding import PartitionSpec as P


NB = 128
F32 = jnp.float32
BF16 = jnp.bfloat16
SPAN = 512
XS = 4
SHIFTED = ((1, 1), (2, 1), (3, 0), (3, 1), (4, 0), (4, 1), (5, 0), (5, 1))


def split(x):
    high = x.astype(BF16)
    return high, (x - high.astype(F32)).astype(BF16)


def mm(a, b):
    return jnp.dot(a, b, preferred_element_type=F32)


def dot3(a, b):
    return mm(a[0], b[0]) + (mm(a[0], b[1]) + mm(a[1], b[0]))


def product(a, b):
    return dot3(split(a), split(b))


def place():
    vec = lax.axis_index("vec")
    return lax.shift_right_logical(vec, 2), vec & 3, lax.axis_index("row") & 1


def assemble(parts, buf, start=0):
    far, near, _ = place()
    width = buf.shape[2]
    for step, part in zip((0, 1, 3, 2), parts):
        x = near ^ step
        for z in range(2):
            buf[(far ^ z) * XS + x] = part[16 * z : 16 * z + 16, start : start + width]


def block(buf, start, width):
    return buf[:, :, start : start + width].reshape(NB, width)


def group_matrix(basis_t, factor):
    return product(basis_t.T, product(factor, basis_t))


def put(refs, index, value):
    high, low = split(value)
    refs[0][index] = high
    refs[1][index] = low


def get(refs, *index):
    return refs[0][index], refs[1][index]


def look_ahead(side, nxt_t, matrix):
    zero = jnp.zeros((NB, NB), F32)
    if side == 0:
        return jnp.concatenate([nxt_t, zero], axis=1) - product(nxt_t, matrix[:NB])
    return jnp.concatenate([zero, nxt_t], axis=1) - product(nxt_t, matrix[NB:])


def spans(body, width):
    def step(c, carry):
        body(pl.ds(pl.multiple_of(c * SPAN, SPAN), SPAN))
        return carry

    lax.fori_loop(0, width // SPAN, step, 0)


def first_payload_kernel(turned, factors, out, shifted, turned_here, factors_here, sem):
    copies = [
        pltpu.make_async_copy(turned, turned_here, sem.at[0]),
        pltpu.make_async_copy(factors, factors_here, sem.at[1]),
    ]
    for copy in copies:
        copy.start()
    for copy in copies:
        copy.wait()
    lay(
        out,
        turned_here[0], *ends(turned_here, 1), factors_here[0, 0], factors_here[0, 1],
        turned_here[1, :, 128:384], factors_here[1, 0], factors_here[1, 1],
    )
    lay(shifted, *(factors_here[r, g] for r, g in SHIFTED))


def lay(out, *parts):
    at = 0
    for part in parts:
        out[:, at : at + part.shape[1]] = part
        at += part.shape[1]


def ends(turned, r):
    return turned[r, :, 0:128], turned[r, :, 384:512]


def rest_payload_kernel(turned, factors, slid, out):
    came = [slid[:, k * NB : (k + 1) * NB] for k in range(8)]
    lay(
        out,
        came[0], turned[2], came[1], factors[2, 0], *ends(turned, 3),
        turned[3, :, 128:384], came[3], factors[3, 0], came[2], turned[4], came[4], came[5], *ends(turned, 5),
        turned[5, :, 128:384], came[6], came[7],
    )


def first_kernel(own, left, right, across, x, ph, pl_, chip, core, nxt_t, buf, lh, ll):
    assemble((own, left, right, across), buf)
    odd = place()[2] == 1
    for side in range(2):
        nxt = block(buf, 512 + side * NB, NB)
        nxt_t[side] = nxt
        matrix = group_matrix(block(buf, side * 256, 256), block(buf, 768 + side * NB, NB))
        put((ph, pl_), side, matrix)
        put((lh, ll), side, look_ahead(side, nxt, matrix))

    def body(cols):
        heads = [
            dot3(get((lh, ll), side), split(x[side * 256 : side * 256 + 256, cols])) for side in range(2)
        ]
        chip[:, cols] = jnp.where(odd, heads[1], heads[0])
        core[:, cols] = jnp.where(odd, heads[0], heads[1])

    spans(body, x.shape[1])


def fill_kernel(own, left, right, across, nxt_t, ph, pl_, x, u, tail, buf, mh, ml):
    assemble((own, left, right, across), buf, 1024)
    put((mh, ml), slice(None), group_matrix(block(buf, 0, 256), block(buf, 256, NB)))
    tail[...] = product(nxt_t[1].T, block(buf, 384, NB))

    def body(cols):
        panels = []
        for side in range(2):
            panel = x[side * 256 : side * 256 + 256, cols]
            panels.append(panel - dot3((ph[side], pl_[side]), split(panel)))
        u[0:128, cols] = panels[0][:NB]
        u[384:512, cols] = panels[1][NB:]
        panel = jnp.concatenate([panels[0][NB:], panels[1][:NB]], axis=0)
        u[128:384, cols] = panel - dot3((mh[...], ml[...]), split(panel))

    spans(body, u.shape[1])


def spread_and_ahead(buf, at, nxt_t, spread, ph, pl_, uh, ul, qh, ql, lh, ll):
    for side in range(2):
        put((uh, ul), side, spread[side])
        factor = block(buf, at + 512 + side * NB, NB)
        nxt = block(buf, at + 768 + side * NB, NB)
        nxt_t[side] = nxt
        matrix = group_matrix(block(buf, at + side * 256, 256), factor)
        put((ph, pl_), side, matrix)
        look = look_ahead(side, nxt, matrix)
        put((lh, ll), side, look)
        put((qh, ql), side, product(look[:, :NB] if side == 0 else look[:, NB:], spread[side]))


def ahead_kernel(own, left, right, across, prev_t, prev_tail, u, *rest):
    ph, pl_, uh, ul, qh, ql, ahead, nxt_t, extra, buf, last_block, lh, ll = rest
    assemble((own, left, right, across), last_block, 3328 - NB)
    for k in range(8):
        extra[:, k * NB : (k + 1) * NB] = last_block[k]
    assemble((own, left, right, across), buf)
    spread = (product(prev_t[0].T, block(buf, 0, NB)), prev_tail[...])
    spread_and_ahead(buf, NB, nxt_t, spread, ph, pl_, uh, ul, qh, ql, lh, ll)

    def body(cols):
        for side in range(2):
            rows = slice(side * 256, side * 256 + 256)
            ahead[side, :, cols] = dot3(get((lh, ll), side), split(u[rows, cols]))

    spans(body, u.shape[1])


def middle_kernel(own, left, right, across, prev_t, u_in, *rest):
    u, ph, pl_, uh, ul, qh, ql, ahead, nxt_t, buf, mh, ml, lh, ll = rest
    assemble((own, left, right, across), buf, 1152)
    put((mh, ml), slice(None), group_matrix(block(buf, 0, 256), block(buf, 256, NB)))
    spread = (product(prev_t[0].T, block(buf, 512, NB)), product(prev_t[1].T, block(buf, 384, NB)))
    spread_and_ahead(buf, 640, nxt_t, spread, ph, pl_, uh, ul, qh, ql, lh, ll)

    def body(cols):
        panel = u_in[128:384, cols]
        panel = panel - dot3((mh[...], ml[...]), split(panel))
        u[128:384, cols] = panel
        top, bottom = u_in[0:128, cols], u_in[384:512, cols]
        u[0:128, cols] = top
        u[384:512, cols] = bottom
        ahead[0, :, cols] = dot3(get((lh, ll), 0), split(jnp.concatenate([top, panel[:NB]], axis=0)))
        ahead[1, :, cols] = dot3(get((lh, ll), 1), split(jnp.concatenate([panel[NB:], bottom], axis=0)))

    spans(body, u.shape[1])


def final_middle_kernel(own, left, right, across, prev_t, u_in, got_chip, got_core, *rest):
    out, uh, ul, buf, mh, ml, rows, sem = rest
    assemble((own, left, right, across), buf, 2816)
    put((mh, ml), slice(None), group_matrix(block(buf, 0, 256), block(buf, 256, NB)))
    copies = []
    for c in range(u_in.shape[1] // SPAN):
        cols = slice(c * SPAN, c * SPAN + SPAN)
        panel = u_in[128:384, cols]
        rows[c] = panel - dot3((mh[...], ml[...]), split(panel))
        copies.append(pltpu.make_async_copy(rows.at[c], out.at[128:384, cols], sem.at[c]))
        copies[-1].start()
    came = jnp.where(place()[2] == 1, got_core[NB:, :], got_chip[NB:, :])
    head = jnp.concatenate([came[:, k * NB : (k + 1) * NB] for k in range(8)], axis=0)
    put((uh, ul), 0, product(prev_t[0].T, head))
    put((uh, ul), 1, product(prev_t[1].T, block(buf, 384, NB)))
    for copy in copies:
        copy.wait()


def next_kernel(own_chip, got_chip, own_core, got_core, qh, ql, ahead, *rest):
    *extra, chip, core = rest
    odd = place()[2]
    for value in extra:
        chip[NB:, :] = value[...]
        core[NB:, :] = value[...]

    def body(cols):
        for own, got, out, side in ((own_chip, got_chip, chip, odd), (own_core, got_core, core, 1 - odd)):
            total = own[:NB, cols] + got[:NB, cols]
            out[:NB, cols] = ahead[side, :, cols] - dot3((qh[side], ql[side]), split(total))

    spans(body, chip.shape[1])


def totals_of(own_chip, got_chip, own_core, got_core, cols):
    odd = place()[2] == 1
    chip = own_chip[:NB, cols] + got_chip[:NB, cols]
    core = own_core[:NB, cols] + got_core[:NB, cols]
    return jnp.where(odd, core, chip), jnp.where(odd, chip, core)


def even_kernel(own_chip, got_chip, own_core, got_core, uh, ul, ph, pl_, u_in, u):
    def body(cols):
        totals = totals_of(own_chip, got_chip, own_core, got_core, cols)
        for side in range(2):
            near = slice(0, 128) if side == 0 else slice(384, 512)
            far = slice(128, 256) if side == 0 else slice(256, 384)
            panel = u_in[near, cols] - dot3((uh[side], ul[side]), split(totals[side]))
            pair = [panel, u_in[far, cols]] if side == 0 else [u_in[far, cols], panel]
            both = jnp.concatenate(pair, axis=0)
            u[side * 256 : side * 256 + 256, cols] = both - dot3((ph[side], pl_[side]), split(both))

    spans(body, u.shape[1])


def last_kernel(own_chip, got_chip, own_core, got_core, uh, ul, u_in, held_out, out, rows, sem):
    del held_out
    copies = []
    for c in range(u_in.shape[1] // SPAN):
        cols = slice(c * SPAN, c * SPAN + SPAN)
        totals = totals_of(own_chip, got_chip, own_core, got_core, cols)
        for side in range(2):
            near = slice(0, 128) if side == 0 else slice(384, 512)
            k = 2 * c + side
            rows[k] = u_in[near, cols] - dot3((uh[side], ul[side]), split(totals[side]))
            copies.append(pltpu.make_async_copy(rows.at[k], out.at[near, cols], sem.at[k]))
            copies[-1].start()
    for copy in copies:
        copy.wait()


def call(kernel, outs, scratch, flops, *args, far=(), far_out=(), sems=0, aliases={}):
    vmem = pl.BlockSpec(memory_space=pltpu.VMEM)
    hbm = pl.BlockSpec(memory_space=pltpu.HBM)
    return pl.pallas_call(
        kernel,
        out_shape=[jax.ShapeDtypeStruct(s, t) for s, t in outs],
        in_specs=[hbm if k in far else vmem for k in range(len(args))],
        out_specs=[hbm if k in far_out else vmem for k in range(len(outs))],
        input_output_aliases=aliases,
        scratch_shapes=[pltpu.VMEM(s, t) for s, t in scratch] + [pltpu.SemaphoreType.DMA((sems,))] * bool(sems),
        cost_estimate=pl.CostEstimate(flops=flops, bytes_accessed=0 if far else 4 << 20, transcendentals=0),
        compiler_params=pltpu.CompilerParams(vmem_limit_bytes=24 << 20),
    )(*args)


def far_half(payload):
    return lax.ppermute(payload, "vec", [(v, v ^ XS) for v in range(2 * XS)])


def near_parts(payload, other):
    both = jnp.concatenate([payload, other], axis=0)
    parts = [lax.ppermute(both, "vec", [(v, v ^ step) for v in range(2 * XS)]) for step in (1, 3, 2)]
    return (both, *parts)


def rounds(eigvecs, reflectors, factors):
    rows = lax.axis_size("row")
    chip_pairs = [p for k in range(1, rows - 1, 2) for p in ((k, k + 1), (k + 1, k))]
    core_pairs = [(k, k ^ 1) for k in range(rows)]
    turned = jnp.transpose(reflectors, (0, 2, 1))
    a, shifted, turned, factors = call(
        first_payload_kernel,
        [((16, 1536), F32), ((16, 1024), F32), (turned.shape, F32), (factors.shape, F32)],
        [],
        1 << 20,
        turned,
        factors,
        far=(0, 1),
        sems=2,
    )
    slid = lax.ppermute(shifted, "row", [(k, k + 1) for k in range(rows - 1)])
    a2 = far_half(a)
    (b,) = call(rest_payload_kernel, [((16, 3328), F32)], [], 1 << 20, turned, factors, slid)
    b2 = far_half(b)
    a = near_parts(a, a2)
    b = near_parts(b, b2)

    width = eigvecs.shape[1]
    whole = ((4 * NB, width), F32)
    strip = ((NB, width), F32)
    pair = ((2, 2 * NB, 2 * NB), BF16)
    small = ((2, NB, NB), BF16)
    ends_t = ((2, NB, NB), F32)
    strips = ((2, NB, width), F32)
    look = ((2, NB, 2 * NB), BF16)
    mid = ((2 * NB, 2 * NB), BF16)

    def held(lanes):
        return ((2 * XS, 16, lanes), F32)

    def swap(chip, core):
        return lax.ppermute(chip, "row", chip_pairs), lax.ppermute(core, "row", core_pairs)

    unit = 2 * NB * NB * width * 3
    p0h, p0l, chip, core, nxt_t = call(
        first_kernel,
        [pair, pair, strip, strip, ends_t],
        [held(1024), look, look],
        4 * unit,
        *a, eigvecs,
    )
    got_chip, got_core = swap(chip, core)
    u, tail = call(
        fill_kernel,
        [whole, ((NB, NB), F32)],
        [held(512), mid, mid],
        12 * unit,
        *a, nxt_t, p0h, p0l, eigvecs,
    )
    ops = [pair, pair, small, small, small, small, strips, ends_t]
    ph, pl_, uh, ul, qh, ql, ahead, nxt_t, extra = call(
        ahead_kernel,
        [*ops, ((16, width), F32)],
        [held(1152), held(NB), look, look],
        4 * unit,
        *b, nxt_t, tail, u,
    )
    longer = ((NB + 16, width), F32)
    new_chip, new_core = call(
        next_kernel, [longer, longer], [], 2 * unit, chip, got_chip, core, got_core, qh, ql, ahead, extra
    )
    far_chip, far_core = swap(new_chip, new_core)
    (u,) = call(even_kernel, [whole], [], 10 * unit, chip, got_chip, core, got_core, uh, ul, ph, pl_, u)
    u, ph, pl_, uh, ul, qh, ql, ahead, nxt_t = call(
        middle_kernel,
        [whole, *ops],
        [held(1664), mid, mid, look, look],
        10 * unit,
        *b, nxt_t, u,
    )
    chip, core = new_chip, new_core
    new_chip, new_core = call(next_kernel, [strip, strip], [], 2 * unit, chip, far_chip, core, far_core, qh, ql, ahead)
    got_chip, got_core = swap(new_chip, new_core)
    (u,) = call(even_kernel, [whole], [], 10 * unit, chip, far_chip, core, far_core, uh, ul, ph, pl_, u)
    out, uh, ul = call(
        final_middle_kernel,
        [whole, small, small],
        [held(512), mid, mid, ((width // SPAN, 2 * NB, SPAN), F32)],
        5 * unit,
        *b, nxt_t, u, far_chip, far_core,
        far_out=(0,),
        sems=width // SPAN,
    )
    (out,) = call(
        last_kernel,
        [whole],
        [((2 * width // SPAN, NB, SPAN), F32)],
        2 * unit,
        new_chip, got_chip, new_core, got_core, uh, ul, u, out,
        far=(7,),
        far_out=(0,),
        sems=2 * width // SPAN,
        aliases={7: 0},
    )
    return out


def solution(mesh):
    return jax.shard_map(
        rounds,
        mesh=mesh,
        in_specs=(P("row", "vec"), P(None, "row", "vec"), P(None, "row", "vec", None)),
        out_specs=P("row", "vec"),
        check_vma=False,
    )
```

time: 103 us -> 104 us (level)
  the two profiles are of different devices: /device:TPU:64 before, /device:TPU:66 now
where the time goes in v1:
time: 104 us
  starting transfers between devices  59.3 us (57%)
  waiting for transfers between devices  20.6 us (20%)
  Pallas kernels  20.1 us (19%)
  local copies, waits for them, and re-layouts  3.42 us (3%)
    ppermute x6, starting transfers between devices, near_parts(): lax.ppermute(both, 'vec', [(v, v ^ step) for v in range(2 * XS)])  20.8 us
    pallas_call x12, Pallas kernels, call(): pl.pallas_call(kernel, out_shape=[jax.ShapeDtypeStruct(s, t) for s, t in...  20.1 us
    ppermute x2, starting transfers between devices, far_half(): return lax.ppermute(payload, 'vec', [(v, v ^ XS) for v in range(2 * XS)])  18.1 us
    ppermute x3, starting transfers between devices, swap(): lax.ppermute(chip, 'row', chip_pairs)  12.6 us
    ppermute x6, waiting for transfers between devices, near_parts(): lax.ppermute(both, 'vec', [(v, v ^ step) for v in range(2 * XS)])  12 us
    ppermute x3, waiting for transfers between devices, swap(): lax.ppermute(chip, 'row', chip_pairs)  5.98 us
    ppermute x3, starting transfers between devices, swap(): lax.ppermute(core, 'row', core_pairs)  5.76 us
    unnamed x7, local copies, waits for them, and re-layouts  3.41 us
  transfers between devices with their start and end apart: 15, of which 6 were waited for; matrix products, arithmetic and copies ran while one was open for 0% of the time, Pallas kernels for 16%

profile of v1, /device:TPU:66, one launch (start us, length us, event | category | flops | bytes accessed | tf_op | source)
XLA Modules:
  0.0 103.7 jit_solution(10551594251538129467)
XLA Ops:
  0.0 0.0 copy-start.1
  0.0 0.9 copy-done.1
  0.9 0.0 copy-start.2
  0.9 0.9 copy-done.2
  1.8 0.4 shard_map.37
  2.2 1.9 %collective-permute-start.6 = (f32[16,1024]{1,0:T(8,128)S(1)}, f32[16,1024]{1,0:T(8,128)S(1)}, u32[]{:S(2)}, u32[]{:S(2)}) collective-permute-start(f32[16,1024]{1,0:T(8,128)S(1)} %get-tuple-element.46), channel_id=1, source_target_pairs={{0,8},{8,16},{16,24},{24,32},{32,40},{40,48},{48,56},{56,64},{64,7... | collective-permute-start | bytes 196616 | tf_op jit(solution)/shard_map/ppermute | solution.py:318
  4.1 10.0 %collective-permute-start = (f32[16,1536]{1,0:T(8,128)S(1)}, f32[16,1536]{1,0:T(8,128)S(1)}, u32[]{:S(2)}, u32[]{:S(2)}) collective-permute-start(f32[16,1536]{1,0:T(8,128)S(1)} %get-tuple-element.41), channel_id=1, source_target_pairs={{0,4},{1,5},{2,6},{3,7},{4,0},{5,1},{6,2},{7,3},{8,12},{9,13},{10,... | collective-permute-start | bytes 294920 | tf_op jit(solution)/shard_map/ppermute | solution.py:294
  14.2 2.6 %collective-permute-done = f32[16,1536]{1,0:T(8,128)S(1)} collective-permute-done((f32[16,1536]{1,0:T(8,128)S(1)}, f32[16,1536]{1,0:T(8,128)S(1)}, u32[]{:S(2)}, u32[]{:S(2)}) %collective-permute-start) | collective-permute-done | bytes 98336 | tf_op jit(solution)/shard_map/ppermute | solution.py:294
  16.8 4.0 %collective-permute-start.3 = (f32[32,1536]{1,0:T(8,128)S(1)}, f32[32,1536]{1,0:T(8,128)S(1)}, u32[]{:S(2)}, u32[]{:S(2)}) collective-permute-start(f32[32,1536]{1,0:T(8,128)S(1)} %constant_dynamic-update-slice_fusion.own), channel_id=1, source_target_pairs={{0,2},{1,3},{2,0},{3,1},{4,6},{5,7},{6,4},{7,5},{8,10},{9,11},{10,... | collective-permute-start | bytes 589832 | tf_op jit(solution)/shard_map/ppermute | solution.py:299
  20.9 1.9 %collective-permute-start.2 = (f32[32,1536]{1,0:T(8,128)S(1)}, f32[32,1536]{1,0:T(8,128)S(1)}, u32[]{:S(2)}, u32[]{:S(2)}) collective-permute-start(f32[32,1536]{1,0:T(8,128)S(1)} %constant_dynamic-update-slice_fusion.own), channel_id=1, source_target_pairs={{0,3},{1,2},{2,1},{3,0},{4,7},{5,6},{6,5},{7,4},{8,11},{9,10},{10,... | collective-permute-start | bytes 589832 | tf_op jit(solution)/shard_map/ppermute | solution.py:299
  22.8 4.5 %collective-permute-start.1 = (f32[32,1536]{1,0:T(8,128)S(1)}, f32[32,1536]{1,0:T(8,128)S(1)}, u32[]{:S(2)}, u32[]{:S(2)}) collective-permute-start(f32[32,1536]{1,0:T(8,128)S(1)} %constant_dynamic-update-slice_fusion.own), channel_id=1, source_target_pairs={{0,1},{1,0},{2,3},{3,2},{4,5},{5,4},{6,7},{7,6},{8,9},{9,8},{10,11... | collective-permute-start | bytes 589832 | tf_op jit(solution)/shard_map/ppermute | solution.py:299
  27.3 0.0 collective-permute-done.6.slid
  27.3 8.1 %collective-permute-start.7 = (f32[16,3328]{1,0:T(8,128)S(1)}, f32[16,3328]{1,0:T(8,128)S(1)}, u32[]{:S(2)}, u32[]{:S(2)}) collective-permute-start(f32[16,3328]{1,0:T(8,128)S(1)} %shard_map.39), channel_id=1, source_target_pairs={{0,4},{1,5},{2,6},{3,7},{4,0},{5,1},{6,2},{7,3},{8,12},{9,13},{10,... | collective-permute-start | bytes 638984 | tf_op jit(solution)/shard_map/ppermute | solution.py:294
  35.4 0.0 collective-permute-done.3.across
  35.4 0.0 collective-permute-done.2.right
  35.4 0.0 collective-permute-done.1.left
  35.4 0.0 copy-start
  35.5 1.6 %copy-done = f32[512,1024]{1,0:T(8,128)S(1)} copy-done((f32[512,1024]{1,0:T(8,128)S(1)}, f32[512,1024]{1,0:T(8,128)}, u32[]{:S(2)}) %copy-start) | copy-done | bytes 2097176
  37.0 2.3 %shard_map.38 = (bf16[2,256,256]{2,1,0:T(8,128)(2,1)S(1)}, bf16[2,256,256]{2,1,0:T(8,128)(2,1)S(1)}, f32[128,1024]{1,0:T(8,128)S(1)}, f32[128,1024]{1,0:T(8,128)S(1)}, f32[2,128,128]{2,1,0:T(8,128)S(1)}) custom-call(f32[32,1536]{1,0:T(8,128)S(1)} %constant_dynamic-update-slice_fusion.own, f32[32,1536]{1,0:T(8,128)S(1)} %collective-permute-done.1.left, ...), custom_call_target="tpu_custom_call" | custom-call | flops 402653184 | bytes 4194304 | tf_op jit(solution)/shard_map/pallas_call | solution.py:281
  39.3 6.4 %collective-permute-start.4 = (f32[128,1024]{1,0:T(8,128)S(1)}, f32[128,1024]{1,0:T(8,128)S(1)}, u32[]{:S(2)}, u32[]{:S(2)}) collective-permute-start(f32[128,1024]{1,0:T(8,128)S(1)} %get-tuple-element.42.own_chip), channel_id=1, source_target_pairs={{8,16},{16,8},{24,32},{32,24},{40,48},{48,40},{56,64},{64,56},{72,... | collective-permute-start | bytes 1572872 | tf_op jit(solution)/shard_map/ppermute | solution.py:339
  45.7 1.9 %collective-permute-start.5 = (f32[128,1024]{1,0:T(8,128)S(1)}, f32[128,1024]{1,0:T(8,128)S(1)}, u32[]{:S(2)}, u32[]{:S(2)}) collective-permute-start(f32[128,1024]{1,0:T(8,128)S(1)} %get-tuple-element.43.own_core), channel_id=1, source_target_pairs={{0,8},{8,0},{16,24},{24,16},{32,40},{40,32},{48,56},{56,48},{64,72... | collective-permute-start | bytes 1572872 | tf_op jit(solution)/shard_map/ppermute | solution.py:339
  47.6 0.0 collective-permute-done.7
  47.7 3.1 %collective-permute-start.10 = (f32[32,3328]{1,0:T(8,128)S(1)}, f32[32,3328]{1,0:T(8,128)S(1)}, u32[]{:S(2)}, u32[]{:S(2)}) collective-permute-start(f32[32,3328]{1,0:T(8,128)S(1)} %pad_maximum_fusion.own), channel_id=1, source_target_pairs={{0,2},{1,3},{2,0},{3,1},{4,6},{5,7},{6,4},{7,5},{8,10},{9,11},{10,... | collective-permute-start | bytes 1277960 | tf_op jit(solution)/shard_map/ppermute | solution.py:299
  50.8 2.4 %collective-permute-start.9 = (f32[32,3328]{1,0:T(8,128)S(1)}, f32[32,3328]{1,0:T(8,128)S(1)}, u32[]{:S(2)}, u32[]{:S(2)}) collective-permute-start(f32[32,3328]{1,0:T(8,128)S(1)} %pad_maximum_fusion.own), channel_id=1, source_target_pairs={{0,3},{1,2},{2,1},{3,0},{4,7},{5,6},{6,5},{7,4},{8,11},{9,10},{10,... | collective-permute-start | bytes 1277960 | tf_op jit(solution)/shard_map/ppermute | solution.py:299
  53.3 4.9 %collective-permute-start.8 = (f32[32,3328]{1,0:T(8,128)S(1)}, f32[32,3328]{1,0:T(8,128)S(1)}, u32[]{:S(2)}, u32[]{:S(2)}) collective-permute-start(f32[32,3328]{1,0:T(8,128)S(1)} %pad_maximum_fusion.own), channel_id=1, source_target_pairs={{0,1},{1,0},{2,3},{3,2},{4,5},{5,4},{6,7},{7,6},{8,9},{9,8},{10,11... | collective-permute-start | bytes 1277960 | tf_op jit(solution)/shard_map/ppermute | solution.py:299
  58.1 2.4 %shard_map.40 = (f32[512,1024]{1,0:T(8,128)S(1)}, f32[128,128]{1,0:T(8,128)S(1)}) custom-call(f32[32,1536]{1,0:T(8,128)S(1)} %constant_dynamic-update-slice_fusion.own, f32[32,1536]{1,0:T(8,128)S(1)} %collective-permute-done.1.left, f32[32,1536]{1,0:T(8,128)S(1)} %collective-permute-done.2.right, f32[32,1536]{1,0:T(8,128)S(1)} %collective-permute-done.3.across, ...), custom_call_target="tpu_custom_call" | custom-call | flops 1207959552 | bytes 4194304 | tf_op jit(solution)/shard_map/pallas_call | solution.py:281
  60.5 3.3 %collective-permute-done.10.across = f32[32,3328]{1,0:T(8,128)S(1)} collective-permute-done((f32[32,3328]{1,0:T(8,128)S(1)}, f32[32,3328]{1,0:T(8,128)S(1)}, u32[]{:S(2)}, u32[]{:S(2)}) %collective-permute-start.10) | collective-permute-done | bytes 426016 | tf_op jit(solution)/shard_map/ppermute | solution.py:299
  63.8 8.6 %collective-permute-done.9.right = f32[32,3328]{1,0:T(8,128)S(1)} collective-permute-done((f32[32,3328]{1,0:T(8,128)S(1)}, f32[32,3328]{1,0:T(8,128)S(1)}, u32[]{:S(2)}, u32[]{:S(2)}) %collective-permute-start.9) | collective-permute-done | bytes 426016 | tf_op jit(solution)/shard_map/ppermute | solution.py:299
  72.4 0.1 collective-permute-done.8.left
  72.5 2.3 %shard_map.41 = (bf16[2,256,256]{2,1,0:T(8,128)(2,1)S(1)}, bf16[2,256,256]{2,1,0:T(8,128)(2,1)S(1)}, bf16[2,128,128]{2,1,0:T(8,128)(2,1)S(1)}, bf16[2,128,128]{2...) custom-call(f32[32,3328]{1,0:T(8,128)S(1)} %pad_maximum_fusion.own, ...), custom_call_target="tpu_custom_call" | custom-call | flops 402653184 | bytes 4194304 | tf_op jit(solution)/shard_map/pallas_call | solution.py:281
  74.8 0.0 collective-permute-done.4.got_chip
  74.8 0.0 collective-permute-done.5.got_core
  74.9 0.7 shard_map.42
  75.6 3.1 %collective-permute-start.11 = (f32[144,1024]{1,0:T(8,128)S(1)}, f32[144,1024]{1,0:T(8,128)S(1)}, u32[]{:S(2)}, u32[]{:S(2)}) collective-permute-start(f32[144,1024]{1,0:T(8,128)S(1)} %get-tuple-element.56.own_chip), channel_id=1, source_target_pairs={{8,16},{16,8},{24,32},{32,24},{40,48},{48,40},{56,64},{64,56},{72,... | collective-permute-start | bytes 1769480 | tf_op jit(solution)/shard_map/ppermute | solution.py:339
  78.7 1.9 %collective-permute-start.12 = (f32[144,1024]{1,0:T(8,128)S(1)}, f32[144,1024]{1,0:T(8,128)S(1)}, u32[]{:S(2)}, u32[]{:S(2)}) collective-permute-start(f32[144,1024]{1,0:T(8,128)S(1)} %get-tuple-element.57.own_core), channel_id=1, source_target_pairs={{0,8},{8,0},{16,24},{24,16},{32,40},{40,32},{48,56},{56,48},{64,72... | collective-permute-start | bytes 1769480 | tf_op jit(solution)/shard_map/ppermute | solution.py:339
  80.7 2.2 %shard_map.43.u_in = f32[512,1024]{1,0:T(8,128)S(1)} custom-call(f32[128,1024]{1,0:T(8,128)S(1)} %get-tuple-element.42.own_chip, f32[128,1024]{1,0:T(8,128)S(1)} %collective-permute-done.4.got_chip, f32[128,1024]{1,0:T(8,128)S(1)} %get-tuple-element.43.own_core, f32[128,1024]{1,0:T(8,128)S(1)} %collective-permute-done.5.got_core, ...), custom_call_target="tpu_custom_call" | custom-call | flops 1006632960 | bytes 4194304 | tf_op jit(solution)/shard_map/pallas_call | solution.py:281
  82.9 3.3 %shard_map.44 = (f32[512,1024]{1,0:T(8,128)S(1)}, bf16[2,256,256]{2,1,0:T(8,128)(2,1)S(1)}, bf16[2,256,256]{2,1,0:T(8,128)(2,1)S(1)}, bf16[2,128,128]{2,1,0:T(8,...) custom-call(f32[32,3328]{1,0:T(8,128)S(1)} %pad_maximum_fusion.own, ...), custom_call_target="tpu_custom_call" | custom-call | flops 1006632960 | bytes 4194304 | tf_op jit(solution)/shard_map/pallas_call | solution.py:281
  86.2 2.8 %collective-permute-done.11.got_chip = f32[144,1024]{1,0:T(8,128)S(1)} collective-permute-done((f32[144,1024]{1,0:T(8,128)S(1)}, f32[144,1024]{1,0:T(8,128)S(1)}, u32[]{:S(2)}, u32[]{:S(2)}) %collective-permute-start.11) | collective-permute-done | bytes 589856 | tf_op jit(solution)/shard_map/ppermute | solution.py:339
  88.9 0.0 collective-permute-done.12.got_core
  88.9 0.7 shard_map.45
  89.7 3.1 %collective-permute-start.13 = (f32[128,1024]{1,0:T(8,128)S(1)}, f32[128,1024]{1,0:T(8,128)S(1)}, u32[]{:S(2)}, u32[]{:S(2)}) collective-permute-start(f32[128,1024]{1,0:T(8,128)S(1)} %get-tuple-element.66.own_chip), channel_id=1, source_target_pairs={{8,16},{16,8},{24,32},{32,24},{40,48},{48,40},{56,64},{64,56},{72,... | collective-permute-start | bytes 1572872 | tf_op jit(solution)/shard_map/ppermute | solution.py:339
  92.8 1.9 %collective-permute-start.14 = (f32[128,1024]{1,0:T(8,128)S(1)}, f32[128,1024]{1,0:T(8,128)S(1)}, u32[]{:S(2)}, u32[]{:S(2)}) collective-permute-start(f32[128,1024]{1,0:T(8,128)S(1)} %get-tuple-element.67.own_core), channel_id=1, source_target_pairs={{0,8},{8,0},{16,24},{24,16},{32,40},{40,32},{48,56},{56,48},{64,72... | collective-permute-start | bytes 1572872 | tf_op jit(solution)/shard_map/ppermute | solution.py:339
  94.7 2.2 %shard_map.46.u_in = f32[512,1024]{1,0:T(8,128)S(1)} custom-call(f32[144,1024]{1,0:T(8,128)S(1)} %get-tuple-element.56.own_chip, f32[144,1024]{1,0:T(8,128)S(1)} %collective-permute-done.11.got_chip, f32[144,1024]{1,0:T(8,128)S(1)} %get-tuple-element.57.own_core, f32[144,1024]{1,0:T(8,128)S(1)} %collective-permute-done.12.got_core, ...), custom_call_target="tpu_custom_call" | custom-call | flops 1006632960 | bytes 4194304 | tf_op jit(solution)/shard_map/pallas_call | solution.py:281
  97.0 2.1 %shard_map.47 = (f32[512,1024]{1,0:T(8,128)}, bf16[2,128,128]{2,1,0:T(8,128)(2,1)S(1)}, bf16[2,128,128]{2,1,0:T(8,128)(2,1)S(1)}) custom-call(f32[32,3328]{1,0:T(8,128)S(1)} %pad_maximum_fusion.own, f32[32,3328]{1,0:T(8,128)S(1)} %collective-permute-done.8.left, f32[32,3328]{1,0:T(8,128)S(1)} %collective-permute-done.9.right, ...), custom_call_target="tpu_custom_call" | custom-call | flops 503316480 | bytes 4194304 | tf_op jit(solution)/shard_map/pallas_call | solution.py:281
  99.0 3.2 %collective-permute-done.13.got_chip = f32[128,1024]{1,0:T(8,128)S(1)} collective-permute-done((f32[128,1024]{1,0:T(8,128)S(1)}, f32[128,1024]{1,0:T(8,128)S(1)}, u32[]{:S(2)}, u32[]{:S(2)}) %collective-permute-start.13) | collective-permute-done | bytes 524320 | tf_op jit(solution)/shard_map/ppermute | solution.py:339
  102.3 0.0 collective-permute-done.14.got_core
  102.3 1.4 %shard_map.48 = f32[512,1024]{1,0:T(8,128)} custom-call(f32[128,1024]{1,0:T(8,128)S(1)} %get-tuple-element.66.own_chip, f32[128,1024]{1,0:T(8,128)S(1)} %collective-permute-done.13.got_chip, f32[128,1024]{1,0:T(8,128)S(1)} %get-tuple-element.67.own_core, f32[128,1024]{1,0:T(8,128)S(1)} %collective-permute-done.14.got_core, ...), custom_call_target="tpu_custom_call", output_to_operand_aliasing={{}: (7, {})} | custom-call | flops 201326592 | tf_op jit(solution)/shard_map/pallas_call | solution.py:281
  (4 shorter events, 0.1 us)
Async XLA Ops:
  0.0 0.9 copy-start.1
  0.9 0.9 copy-start.2
  2.2 25.1 %collective-permute-start.6 = (f32[16,1024]{1,0:T(8,128)S(1)}, f32[16,1024]{1,0:T(8,128)S(1)}, u32[]{:S(2)}, u32[]{:S(2)}) collective-permute-start(f32[16,1024]{1,0:T(8,128)S(1)} %get-tuple-element.46), channel_id=1, source_target_pairs={{0,8},{8,16},{16,24},{24,32},{32,40},{40,48},{48,56},{56,64},{64,7... | collective-permute-start | bytes 196616 | tf_op jit(solution)/shard_map/ppermute | solution.py:318
  4.1 12.7 %collective-permute-start = (f32[16,1536]{1,0:T(8,128)S(1)}, f32[16,1536]{1,0:T(8,128)S(1)}, u32[]{:S(2)}, u32[]{:S(2)}) collective-permute-start(f32[16,1536]{1,0:T(8,128)S(1)} %get-tuple-element.41), channel_id=1, source_target_pairs={{0,4},{1,5},{2,6},{3,7},{4,0},{5,1},{6,2},{7,3},{8,12},{9,13},{10,... | collective-permute-start | bytes 294920 | tf_op jit(solution)/shard_map/ppermute | solution.py:294
  16.8 18.6 %collective-permute-start.3 = (f32[32,1536]{1,0:T(8,128)S(1)}, f32[32,1536]{1,0:T(8,128)S(1)}, u32[]{:S(2)}, u32[]{:S(2)}) collective-permute-start(f32[32,1536]{1,0:T(8,128)S(1)} %constant_dynamic-update-slice_fusion.own), channel_id=1, source_target_pairs={{0,2},{1,3},{2,0},{3,1},{4,6},{5,7},{6,4},{7,5},{8,10},{9,11},{10,... | collective-permute-start | bytes 589832 | tf_op jit(solution)/shard_map/ppermute | solution.py:299
  20.9 14.6 %collective-permute-start.2 = (f32[32,1536]{1,0:T(8,128)S(1)}, f32[32,1536]{1,0:T(8,128)S(1)}, u32[]{:S(2)}, u32[]{:S(2)}) collective-permute-start(f32[32,1536]{1,0:T(8,128)S(1)} %constant_dynamic-update-slice_fusion.own), channel_id=1, source_target_pairs={{0,3},{1,2},{2,1},{3,0},{4,7},{5,6},{6,5},{7,4},{8,11},{9,10},{10,... | collective-permute-start | bytes 589832 | tf_op jit(solution)/shard_map/ppermute | solution.py:299
  22.8 12.7 %collective-permute-start.1 = (f32[32,1536]{1,0:T(8,128)S(1)}, f32[32,1536]{1,0:T(8,128)S(1)}, u32[]{:S(2)}, u32[]{:S(2)}) collective-permute-start(f32[32,1536]{1,0:T(8,128)S(1)} %constant_dynamic-update-slice_fusion.own), channel_id=1, source_target_pairs={{0,1},{1,0},{2,3},{3,2},{4,5},{5,4},{6,7},{7,6},{8,9},{9,8},{10,11... | collective-permute-start | bytes 589832 | tf_op jit(solution)/shard_map/ppermute | solution.py:299
  27.3 20.3 %collective-permute-start.7 = (f32[16,3328]{1,0:T(8,128)S(1)}, f32[16,3328]{1,0:T(8,128)S(1)}, u32[]{:S(2)}, u32[]{:S(2)}) collective-permute-start(f32[16,3328]{1,0:T(8,128)S(1)} %shard_map.39), channel_id=1, source_target_pairs={{0,4},{1,5},{2,6},{3,7},{4,0},{5,1},{6,2},{7,3},{8,12},{9,13},{10,... | collective-permute-start | bytes 638984 | tf_op jit(solution)/shard_map/ppermute | solution.py:294
  35.4 1.6 %copy-start = (f32[512,1024]{1,0:T(8,128)S(1)}, f32[512,1024]{1,0:T(8,128)}, u32[]{:S(2)}) copy-start(f32[512,1024]{1,0:T(8,128)} %x.3) | copy-start | bytes 6291460
  39.3 35.5 %collective-permute-start.4 = (f32[128,1024]{1,0:T(8,128)S(1)}, f32[128,1024]{1,0:T(8,128)S(1)}, u32[]{:S(2)}, u32[]{:S(2)}) collective-permute-start(f32[128,1024]{1,0:T(8,128)S(1)} %get-tuple-element.42.own_chip), channel_id=1, source_target_pairs={{8,16},{16,8},{24,32},{32,24},{40,48},{48,40},{56,64},{64,56},{72,... | collective-permute-start | bytes 1572872 | tf_op jit(solution)/shard_map/ppermute | solution.py:339
  45.7 29.2 %collective-permute-start.5 = (f32[128,1024]{1,0:T(8,128)S(1)}, f32[128,1024]{1,0:T(8,128)S(1)}, u32[]{:S(2)}, u32[]{:S(2)}) collective-permute-start(f32[128,1024]{1,0:T(8,128)S(1)} %get-tuple-element.43.own_core), channel_id=1, source_target_pairs={{0,8},{8,0},{16,24},{24,16},{32,40},{40,32},{48,56},{56,48},{64,72... | collective-permute-start | bytes 1572872 | tf_op jit(solution)/shard_map/ppermute | solution.py:339
  47.7 16.1 %collective-permute-start.10 = (f32[32,3328]{1,0:T(8,128)S(1)}, f32[32,3328]{1,0:T(8,128)S(1)}, u32[]{:S(2)}, u32[]{:S(2)}) collective-permute-start(f32[32,3328]{1,0:T(8,128)S(1)} %pad_maximum_fusion.own), channel_id=1, source_target_pairs={{0,2},{1,3},{2,0},{3,1},{4,6},{5,7},{6,4},{7,5},{8,10},{9,11},{10,... | collective-permute-start | bytes 1277960 | tf_op jit(solution)/shard_map/ppermute | solution.py:299
  50.8 21.6 %collective-permute-start.9 = (f32[32,3328]{1,0:T(8,128)S(1)}, f32[32,3328]{1,0:T(8,128)S(1)}, u32[]{:S(2)}, u32[]{:S(2)}) collective-permute-start(f32[32,3328]{1,0:T(8,128)S(1)} %pad_maximum_fusion.own), channel_id=1, source_target_pairs={{0,3},{1,2},{2,1},{3,0},{4,7},{5,6},{6,5},{7,4},{8,11},{9,10},{10,... | collective-permute-start | bytes 1277960 | tf_op jit(solution)/shard_map/ppermute | solution.py:299
  53.3 19.2 %collective-permute-start.8 = (f32[32,3328]{1,0:T(8,128)S(1)}, f32[32,3328]{1,0:T(8,128)S(1)}, u32[]{:S(2)}, u32[]{:S(2)}) collective-permute-start(f32[32,3328]{1,0:T(8,128)S(1)} %pad_maximum_fusion.own), channel_id=1, source_target_pairs={{0,1},{1,0},{2,3},{3,2},{4,5},{5,4},{6,7},{7,6},{8,9},{9,8},{10,11... | collective-permute-start | bytes 1277960 | tf_op jit(solution)/shard_map/ppermute | solution.py:299
  75.6 13.3 %collective-permute-start.11 = (f32[144,1024]{1,0:T(8,128)S(1)}, f32[144,1024]{1,0:T(8,128)S(1)}, u32[]{:S(2)}, u32[]{:S(2)}) collective-permute-start(f32[144,1024]{1,0:T(8,128)S(1)} %get-tuple-element.56.own_chip), channel_id=1, source_target_pairs={{8,16},{16,8},{24,32},{32,24},{40,48},{48,40},{56,64},{64,56},{72,... | collective-permute-start | bytes 1769480 | tf_op jit(solution)/shard_map/ppermute | solution.py:339
  78.7 10.2 %collective-permute-start.12 = (f32[144,1024]{1,0:T(8,128)S(1)}, f32[144,1024]{1,0:T(8,128)S(1)}, u32[]{:S(2)}, u32[]{:S(2)}) collective-permute-start(f32[144,1024]{1,0:T(8,128)S(1)} %get-tuple-element.57.own_core), channel_id=1, source_target_pairs={{0,8},{8,0},{16,24},{24,16},{32,40},{40,32},{48,56},{56,48},{64,72... | collective-permute-start | bytes 1769480 | tf_op jit(solution)/shard_map/ppermute | solution.py:339
  89.7 12.6 %collective-permute-start.13 = (f32[128,1024]{1,0:T(8,128)S(1)}, f32[128,1024]{1,0:T(8,128)S(1)}, u32[]{:S(2)}, u32[]{:S(2)}) collective-permute-start(f32[128,1024]{1,0:T(8,128)S(1)} %get-tuple-element.66.own_chip), channel_id=1, source_target_pairs={{8,16},{16,8},{24,32},{32,24},{40,48},{48,40},{56,64},{64,56},{72,... | collective-permute-start | bytes 1572872 | tf_op jit(solution)/shard_map/ppermute | solution.py:339
  92.8 9.5 %collective-permute-start.14 = (f32[128,1024]{1,0:T(8,128)S(1)}, f32[128,1024]{1,0:T(8,128)S(1)}, u32[]{:S(2)}, u32[]{:S(2)}) collective-permute-start(f32[128,1024]{1,0:T(8,128)S(1)} %get-tuple-element.67.own_core), channel_id=1, source_target_pairs={{0,8},{8,0},{16,24},{24,16},{32,40},{40,32},{48,56},{56,48},{64,72... | collective-permute-start | bytes 1572872 | tf_op jit(solution)/shard_map/ppermute | solution.py:339

commit v2 on v1

v2 whole, which is shorter than its diff:
```python
import jax
import jax.numpy as jnp
from jax import lax
from jax.experimental import pallas as pl
from jax.experimental.pallas import tpu as pltpu
from jax.sharding import PartitionSpec as P


NB = 128
F32 = jnp.float32
BF16 = jnp.bfloat16
SPAN = 512
XS = 4
SHIFTED = ((1, 1), (2, 1), (3, 0), (3, 1), (4, 0), (4, 1), (5, 0), (5, 1))


def split(x):
    high = x.astype(BF16)
    return high, (x - high.astype(F32)).astype(BF16)


def mm(a, b):
    return jnp.dot(a, b, preferred_element_type=F32)


def dot3(a, b):
    return mm(a[0], b[0]) + (mm(a[0], b[1]) + mm(a[1], b[0]))


def product(a, b):
    return dot3(split(a), split(b))


def place():
    vec = lax.axis_index("vec")
    return lax.shift_right_logical(vec, 2), vec & 3, lax.axis_index("row") & 1


def assemble(parts, buf, start=0):
    far, near, _ = place()
    width = buf.shape[2]
    for step, part in zip((0, 1, 3, 2), parts):
        x = near ^ step
        for z in range(2):
            buf[(far ^ z) * XS + x] = part[16 * z : 16 * z + 16, start : start + width]


def block(buf, start, width):
    return buf[:, :, start : start + width].reshape(NB, width)


def group_matrix(basis_t, factor):
    return product(basis_t.T, product(factor, basis_t))


def put(refs, index, value):
    high, low = split(value)
    refs[0][index] = high
    refs[1][index] = low


def get(refs, *index):
    return refs[0][index], refs[1][index]


def look_ahead(side, nxt_t, matrix):
    zero = jnp.zeros((NB, NB), F32)
    if side == 0:
        return jnp.concatenate([nxt_t, zero], axis=1) - product(nxt_t, matrix[:NB])
    return jnp.concatenate([zero, nxt_t], axis=1) - product(nxt_t, matrix[NB:])


def spans(body, width):
    def step(c, carry):
        body(pl.ds(pl.multiple_of(c * SPAN, SPAN), SPAN))
        return carry

    lax.fori_loop(0, width // SPAN, step, 0)


def lay(out, *parts):
    at = 0
    for part in parts:
        out[:, at : at + part.shape[1]] = part
        at += part.shape[1]


def ends(turned, r):
    return turned[r, :, 0:128], turned[r, :, 384:512]


def shift_kernel(factors, shifted):
    lay(shifted, *(factors[r, g] for r, g in SHIFTED))


def first_payload_kernel(turned, factors, out):
    lay(
        out,
        turned[0], *ends(turned, 1), factors[0, 0], factors[0, 1],
        turned[1, :, 128:384], factors[1, 0], factors[1, 1],
    )


def rest_payload_kernel(turned, factors, slid, out):
    came = [slid[:, k * NB : (k + 1) * NB] for k in range(8)]
    lay(
        out,
        came[0], came[1], factors[2, 0], *ends(turned, 3),
        turned[3, :, 128:384], came[3], factors[3, 0], came[2], turned[4], came[4], came[5], *ends(turned, 5),
        turned[5, :, 128:384], came[6], came[7], turned[2],
    )


def first_kernel(own, left, right, across, x, ph, pl_, chip, core, nxt_t, buf, lh, ll):
    assemble((own, left, right, across), buf)
    odd = place()[2] == 1
    for side in range(2):
        nxt = block(buf, 512 + side * NB, NB)
        nxt_t[side] = nxt
        matrix = group_matrix(block(buf, side * 256, 256), block(buf, 768 + side * NB, NB))
        put((ph, pl_), side, matrix)
        put((lh, ll), side, look_ahead(side, nxt, matrix))

    def body(cols):
        heads = [
            dot3(get((lh, ll), side), split(x[side * 256 : side * 256 + 256, cols])) for side in range(2)
        ]
        chip[:, cols] = jnp.where(odd, heads[1], heads[0])
        core[:, cols] = jnp.where(odd, heads[0], heads[1])

    spans(body, x.shape[1])


def fill_kernel(own, left, right, across, nxt_t, ph, pl_, x, u, tail, buf, mh, ml):
    assemble((own, left, right, across), buf, 1024)
    put((mh, ml), slice(None), group_matrix(block(buf, 0, 256), block(buf, 256, NB)))
    tail[...] = product(nxt_t[1].T, block(buf, 384, NB))

    def body(cols):
        panels = []
        for side in range(2):
            panel = x[side * 256 : side * 256 + 256, cols]
            panels.append(panel - dot3((ph[side], pl_[side]), split(panel)))
        u[0:128, cols] = panels[0][:NB]
        u[384:512, cols] = panels[1][NB:]
        panel = jnp.concatenate([panels[0][NB:], panels[1][:NB]], axis=0)
        u[128:384, cols] = panel - dot3((mh[...], ml[...]), split(panel))

    spans(body, u.shape[1])


def packed(value):
    return jnp.concatenate([value[16 * k : 16 * k + 16] for k in range(8)], axis=1)


def unpacked(value):
    return jnp.concatenate([value[:, k * NB : (k + 1) * NB] for k in range(8)], axis=0)


def chosen(odd, values):
    return jnp.where(odd, values[1], values[0]), jnp.where(odd, values[0], values[1])


def spread_and_ahead(basis, buf, at, nxt_t, spread, chip, core, core_at, ph, pl_, uh, ul, lh, ll):
    tops = []
    for side in range(2):
        put((uh, ul), side, spread[side])
        nxt = block(buf, at + 256 + side * NB, NB)
        nxt_t[side] = nxt
        matrix = group_matrix(block(basis, side * 256, 256), block(buf, at + side * NB, NB))
        put((ph, pl_), side, matrix)
        look = look_ahead(side, nxt, matrix)
        put((lh, ll), side, look)
        tops.append(packed(product(look[:, :NB] if side == 0 else look[:, NB:], spread[side])))
    first, second = chosen(place()[2] == 1, tops)
    chip[NB : NB + 16, :] = first
    core[core_at + NB : core_at + NB + 16, :] = second


def ahead_kernel(prev_t, prev_tail, u, own, left, right, across, *rest):
    ph, pl_, uh, ul, chip, core, nxt_t, basis, buf, last_block, lh, ll = rest
    parts = (own, left, right, across)
    assemble(parts, basis, 2816)
    assemble(parts, buf)
    assemble(parts, last_block, 2816 - NB)
    odd = place()[2] == 1
    for k in range(8):
        chip[NB + 16 :, k * NB : (k + 1) * NB] = last_block[k]
        core[NB + 16 :, k * NB : (k + 1) * NB] = last_block[k]
    spread = (product(prev_t[0].T, block(buf, 0, NB)), prev_tail[...])
    spread_and_ahead(basis, buf, NB, nxt_t, spread, chip, core, 0, ph, pl_, uh, ul, lh, ll)

    def body(cols):
        heads = [dot3(get((lh, ll), side), split(u[side * 256 : side * 256 + 256, cols])) for side in range(2)]
        chip[:NB, cols], core[:NB, cols] = chosen(odd, heads)

    spans(body, u.shape[1])


def middle_kernel(own, left, right, across, prev_t, u_in, prev_core, *rest):
    u, ph, pl_, uh, ul, chip, core, nxt_t, buf, basis, tips, mh, ml, lh, ll = rest
    parts = (own, left, right, across)
    assemble(parts, buf, 640)
    assemble(parts, basis, 1280)
    assemble(parts, tips, 1792)
    odd = place()[2] == 1
    start = prev_core.shape[0]
    put((mh, ml), slice(None), group_matrix(block(buf, 0, 256), block(buf, 256, NB)))
    spread = (product(prev_t[0].T, block(buf, 512, NB)), product(prev_t[1].T, block(buf, 384, NB)))
    spread_and_ahead(basis, tips, 0, nxt_t, spread, chip, core, start, ph, pl_, uh, ul, lh, ll)

    def body(cols):
        core[:start, cols] = prev_core[:, cols]
        panel = u_in[128:384, cols]
        panel = panel - dot3((mh[...], ml[...]), split(panel))
        u[128:384, cols] = panel
        top, bottom = u_in[0:128, cols], u_in[384:512, cols]
        u[0:128, cols] = top
        u[384:512, cols] = bottom
        heads = [
            dot3(get((lh, ll), 0), split(jnp.concatenate([top, panel[:NB]], axis=0))),
            dot3(get((lh, ll), 1), split(jnp.concatenate([panel[NB:], bottom], axis=0))),
        ]
        chip[:NB, cols], core[start : start + NB, cols] = chosen(odd, heads)

    spans(body, u.shape[1])


def both_sides(own_chip, got_chip, own_core, got_core, core_at, rows, cols):
    odd = place()[2] == 1
    lower = slice(core_at + rows.start, core_at + rows.stop)
    chip = own_chip[rows, cols] + got_chip[rows, cols]
    core = own_core[lower, cols] + got_core[lower, cols]
    return chosen(odd, (chip, core))


STRIP = slice(0, NB)
OPERATOR = slice(NB, NB + 16)
BLOCK = slice(NB + 16, NB + 32)
EVERY = slice(None)


def even_kernel(chip1, got1, core1, got_core1, uh, ul, ph, pl_, u_in, u):
    def body(cols):
        totals = both_sides(chip1, got1, core1, got_core1, 0, STRIP, cols)
        straddle_and_even(totals, uh, ul, ph, pl_, u_in, u, cols)

    spans(body, u.shape[1])


def straddle_and_even(totals, uh, ul, ph, pl_, u_in, u, cols):
    for side in range(2):
        near = slice(0, 128) if side == 0 else slice(384, 512)
        far = slice(128, 256) if side == 0 else slice(256, 384)
        panel = u_in[near, cols] - dot3((uh[side], ul[side]), split(totals[side]))
        pair = [panel, u_in[far, cols]] if side == 0 else [u_in[far, cols], panel]
        both = jnp.concatenate(pair, axis=0)
        u[side * 256 : side * 256 + 256, cols] = both - dot3((ph[side], pl_[side]), split(both))


def late_even_kernel(chip1, got1, core1, got_core1, chip3, got3, core35, got_core35, uh, ul, ph, pl_, u_in, *rest):
    u, sums, qh, ql = rest
    three = (chip3, got3, core35, got_core35)
    for side, value in enumerate(both_sides(*three, 0, OPERATOR, EVERY)):
        put((qh, ql), side, unpacked(value))

    def body(cols):
        ones = both_sides(chip1, got1, core1, got_core1, 0, STRIP, cols)
        threes = both_sides(*three, 0, STRIP, cols)
        totals = [threes[side] - dot3(get((qh, ql), side), split(ones[side])) for side in range(2)]
        for side in range(2):
            sums[side, :, cols] = totals[side]
        straddle_and_even(totals, uh, ul, ph, pl_, u_in, u, cols)

    spans(body, u.shape[1])


def final_middle_kernel(own, left, right, across, prev_t, u_in, got3, got_core35, *rest):
    out, uh, ul, buf, mh, ml, rows, sem = rest
    assemble((own, left, right, across), buf, 2304)
    put((mh, ml), slice(None), group_matrix(block(buf, 0, 256), block(buf, 256, NB)))
    copies = []
    for c in range(u_in.shape[1] // SPAN):
        cols = slice(c * SPAN, c * SPAN + SPAN)
        panel = u_in[128:384, cols]
        rows[c] = panel - dot3((mh[...], ml[...]), split(panel))
        copies.append(pltpu.make_async_copy(rows.at[c], out.at[128:384, cols], sem.at[c]))
        copies[-1].start()
    head = unpacked(jnp.where(place()[2] == 1, got_core35[BLOCK, :], got3[BLOCK, :]))
    put((uh, ul), 0, product(prev_t[0].T, head))
    put((uh, ul), 1, product(prev_t[1].T, block(buf, 384, NB)))
    for copy in copies:
        copy.wait()


def last_kernel(chip5, got5, core35, got_core35, sums, uh, ul, u_in, held_out, out, qh, ql, rows, sem):
    del held_out
    start = core35.shape[0] - chip5.shape[0]
    five = (chip5, got5, core35, got_core35)
    for side, value in enumerate(both_sides(*five, start, OPERATOR, EVERY)):
        put((qh, ql), side, unpacked(value))
    copies = []
    for c in range(u_in.shape[1] // SPAN):
        cols = slice(c * SPAN, c * SPAN + SPAN)
        fives = both_sides(*five, start, STRIP, cols)
        for side in range(2):
            near = slice(0, 128) if side == 0 else slice(384, 512)
            k = 2 * c + side
            total = fives[side] - dot3(get((qh, ql), side), split(sums[side, :, cols]))
            rows[k] = u_in[near, cols] - dot3((uh[side], ul[side]), split(total))
            copies.append(pltpu.make_async_copy(rows.at[k], out.at[near, cols], sem.at[k]))
            copies[-1].start()
    for copy in copies:
        copy.wait()


def call(kernel, outs, scratch, flops, *args, far=(), far_out=(), sems=0, aliases={}):
    vmem = pl.BlockSpec(memory_space=pltpu.VMEM)
    hbm = pl.BlockSpec(memory_space=pltpu.HBM)
    return pl.pallas_call(
        kernel,
        out_shape=[jax.ShapeDtypeStruct(s, t) for s, t in outs],
        in_specs=[hbm if k in far else vmem for k in range(len(args))],
        out_specs=[hbm if k in far_out else vmem for k in range(len(outs))],
        input_output_aliases=aliases,
        scratch_shapes=[pltpu.VMEM(s, t) for s, t in scratch] + [pltpu.SemaphoreType.DMA((sems,))] * bool(sems),
        cost_estimate=pl.CostEstimate(flops=flops, bytes_accessed=0 if far else 4 << 20, transcendentals=0),
        compiler_params=pltpu.CompilerParams(vmem_limit_bytes=24 << 20),
    )(*args)


def far_half(payload):
    return lax.ppermute(payload, "vec", [(v, v ^ XS) for v in range(2 * XS)])


def near_parts(payload, other):
    both = jnp.concatenate([payload, other], axis=0)
    parts = [lax.ppermute(both, "vec", [(v, v ^ step) for v in range(2 * XS)]) for step in (1, 3, 2)]
    return (both, *parts)


def rounds(eigvecs, reflectors, factors):
    rows = lax.axis_size("row")
    chip_pairs = [p for k in range(1, rows - 1, 2) for p in ((k, k + 1), (k + 1, k))]
    core_pairs = [(k, k ^ 1) for k in range(rows)]
    turned = jnp.transpose(reflectors, (0, 2, 1))
    (shifted,) = call(shift_kernel, [((16, 1024), F32)], [], 1 << 20, factors)
    slid = lax.ppermute(shifted, "row", [(k, k + 1) for k in range(rows - 1)])
    (a,) = call(first_payload_kernel, [((16, 1536), F32)], [], 1 << 20, turned, factors)
    a2 = far_half(a)
    (b,) = call(rest_payload_kernel, [((16, 3328), F32)], [], 1 << 20, turned, factors, slid)
    b2 = far_half(b)
    a = near_parts(a, a2)
    b = near_parts(b, b2)

    width = eigvecs.shape[1]
    whole = ((4 * NB, width), F32)
    strip = ((NB, width), F32)
    pair = ((2, 2 * NB, 2 * NB), BF16)
    small = ((2, NB, NB), BF16)
    ends_t = ((2, NB, NB), F32)
    strips = ((2, NB, width), F32)
    look = ((2, NB, 2 * NB), BF16)
    mid = ((2 * NB, 2 * NB), BF16)

    def held(lanes):
        return ((2 * XS, 16, lanes), F32)

    def across_chips(value):
        return lax.ppermute(value, "row", chip_pairs)

    def across_cores(value):
        return lax.ppermute(value, "row", core_pairs)

    unit = 2 * NB * NB * width * 3
    p0h, p0l, chip, core, nxt_t = call(
        first_kernel,
        [pair, pair, strip, strip, ends_t],
        [held(1024), look, look],
        4 * unit,
        *a, eigvecs,
    )
    ones = (chip, across_chips(chip), core, across_cores(core))
    u, tail = call(
        fill_kernel,
        [whole, ((NB, NB), F32)],
        [held(512), mid, mid],
        12 * unit,
        *a, nxt_t, p0h, p0l, eigvecs,
    )
    long = ((NB + 32, width), F32)
    shorter = ((NB + 16, width), F32)
    double = ((2 * NB + 48, width), F32)
    ph, pl_, uh, ul, chip3, core3, nxt_t = call(
        ahead_kernel,
        [pair, pair, small, small, long, long, ends_t],
        [held(512), held(640), held(NB), look, look],
        4 * unit,
        nxt_t, tail, u, *b,
    )
    got3 = across_chips(chip3)
    (u,) = call(even_kernel, [whole], [], 10 * unit, *ones, uh, ul, ph, pl_, u)
    u, ph, pl_, uh, ul, chip5, core35, nxt_t = call(
        middle_kernel,
        [whole, pair, pair, small, small, shorter, double, ends_t],
        [held(640), held(512), held(512), mid, mid, look, look],
        10 * unit,
        *b, nxt_t, u, core3,
    )
    got5 = across_chips(chip5)
    got_core35 = across_cores(core35)
    u, sums = call(
        late_even_kernel,
        [whole, strips],
        [small, small],
        12 * unit,
        *ones, chip3, got3, core35, got_core35, uh, ul, ph, pl_, u,
    )
    out, uh, ul = call(
        final_middle_kernel,
        [whole, small, small],
        [held(512), mid, mid, ((width // SPAN, 2 * NB, SPAN), F32)],
        5 * unit,
        *b, nxt_t, u, got3, got_core35,
        far_out=(0,),
        sems=width // SPAN,
    )
    (out,) = call(
        last_kernel,
        [whole],
        [small, small, ((2 * width // SPAN, NB, SPAN), F32)],
        4 * unit,
        chip5, got5, core35, got_core35, sums, uh, ul, u, out,
        far=(8,),
        far_out=(0,),
        sems=2 * width // SPAN,
        aliases={8: 0},
    )
    return out


def solution(mesh):
    return jax.shard_map(
        rounds,
        mesh=mesh,
        in_specs=(P("row", "vec"), P(None, "row", "vec"), P(None, "row", "vec", None)),
        out_specs=P("row", "vec"),
        check_vma=False,
    )
```

time: 104 us -> 105 us (level)
  the two profiles are of different devices: /device:TPU:66 before, /device:TPU:57 now
where the time goes in v2:
time: 105 us
  starting transfers between devices  59.2 us (56%)
  waiting for transfers between devices  21.4 us (20%)
  Pallas kernels  19.6 us (19%)
  local copies, waits for them, and re-layouts  4.33 us (4%)
    pallas_call x11, Pallas kernels, call(): pl.pallas_call(kernel, out_shape=[jax.ShapeDtypeStruct(s, t) for s, t in...  19.6 us
    ppermute x6, starting transfers between devices, near_parts(): lax.ppermute(both, 'vec', [(v, v ^ step) for v in range(2 * XS)])  18.7 us
    ppermute x2, starting transfers between devices, far_half(): return lax.ppermute(payload, 'vec', [(v, v ^ XS) for v in range(2 * XS)])  16.8 us
    ppermute x6, waiting for transfers between devices, near_parts(): lax.ppermute(both, 'vec', [(v, v ^ step) for v in range(2 * XS)])  13.5 us
    ppermute x2, starting transfers between devices, across_cores(): return lax.ppermute(value, 'row', core_pairs)  10.6 us
    ppermute x3, starting transfers between devices, across_chips(): return lax.ppermute(value, 'row', chip_pairs)  9.96 us
    ppermute x3, waiting for transfers between devices, across_chips(): return lax.ppermute(value, 'row', chip_pairs)  7.8 us
    unnamed x8, local copies, waits for them, and re-layouts  4.33 us
  transfers between devices with their start and end apart: 14, of which 4 were waited for; matrix products, arithmetic and copies ran while one was open for 0% of the time, Pallas kernels for 11%

profile of v2, /device:TPU:57, one launch (start us, length us, event | category | flops | bytes accessed | tf_op | source)
XLA Modules:
  0.0 104.8 jit_solution(2459202454325236590)
XLA Ops:
  0.0 0.0 copy-start.1
  0.0 0.9 copy-done.1
  0.9 0.0 copy-start.2
  0.9 0.9 copy-done.2
  1.8 10.6 %collective-permute-start.5 = (f32[16,1536]{1,0:T(8,128)S(1)}, f32[16,1536]{1,0:T(8,128)S(1)}, u32[]{:S(2)}, u32[]{:S(2)}) collective-permute-start(f32[16,1536]{1,0:T(8,128)S(1)} %shard_map.39), channel_id=1, source_target_pairs={{0,4},{1,5},{2,6},{3,7},{4,0},{5,1},{6,2},{7,3},{8,12},{9,13},{10,... | collective-permute-start | bytes 294920 | tf_op jit(solution)/shard_map/ppermute | solution.py:333
  12.5 3.1 %collective-permute-start = (f32[16,1024]{1,0:T(8,128)S(1)}, f32[16,1024]{1,0:T(8,128)S(1)}, u32[]{:S(2)}, u32[]{:S(2)}) collective-permute-start(f32[16,1024]{1,0:T(8,128)S(1)} %shard_map.37), channel_id=1, source_target_pairs={{0,8},{8,16},{16,24},{24,32},{32,40},{40,48},{48,56},{56,64},{64,7... | collective-permute-start | bytes 196616 | tf_op jit(solution)/shard_map/ppermute | solution.py:348
  15.6 0.0 collective-permute-done.5
  15.7 3.1 %collective-permute-start.6 = (f32[32,1536]{1,0:T(8,128)S(1)}, f32[32,1536]{1,0:T(8,128)S(1)}, u32[]{:S(2)}, u32[]{:S(2)}) collective-permute-start(f32[32,1536]{1,0:T(8,128)S(1)} %pad_maximum_fusion.1.own), channel_id=1, source_target_pairs={{0,1},{1,0},{2,3},{3,2},{4,5},{5,4},{6,7},{7,6},{8,9},{9,8},{10,11... | collective-permute-start | bytes 589832 | tf_op jit(solution)/shard_map/ppermute | solution.py:338
  18.8 3.7 %collective-permute-start.7 = (f32[32,1536]{1,0:T(8,128)S(1)}, f32[32,1536]{1,0:T(8,128)S(1)}, u32[]{:S(2)}, u32[]{:S(2)}) collective-permute-start(f32[32,1536]{1,0:T(8,128)S(1)} %pad_maximum_fusion.1.own), channel_id=1, source_target_pairs={{0,3},{1,2},{2,1},{3,0},{4,7},{5,6},{6,5},{7,4},{8,11},{9,10},{10,... | collective-permute-start | bytes 589832 | tf_op jit(solution)/shard_map/ppermute | solution.py:338
  22.5 2.6 %collective-permute-start.8 = (f32[32,1536]{1,0:T(8,128)S(1)}, f32[32,1536]{1,0:T(8,128)S(1)}, u32[]{:S(2)}, u32[]{:S(2)}) collective-permute-start(f32[32,1536]{1,0:T(8,128)S(1)} %pad_maximum_fusion.1.own), channel_id=1, source_target_pairs={{0,2},{1,3},{2,0},{3,1},{4,6},{5,7},{6,4},{7,5},{8,10},{9,11},{10,... | collective-permute-start | bytes 589832 | tf_op jit(solution)/shard_map/ppermute | solution.py:338
  25.1 0.0 collective-permute-done.slid
  25.1 0.0 copy-start.3
  25.1 0.9 copy-done.3
  26.1 6.2 %collective-permute-start.1 = (f32[16,3328]{1,0:T(8,128)S(1)}, f32[16,3328]{1,0:T(8,128)S(1)}, u32[]{:S(2)}, u32[]{:S(2)}) collective-permute-start(f32[16,3328]{1,0:T(8,128)S(1)} %shard_map.38), channel_id=1, source_target_pairs={{0,4},{1,5},{2,6},{3,7},{4,0},{5,1},{6,2},{7,3},{8,12},{9,13},{10,... | collective-permute-start | bytes 638984 | tf_op jit(solution)/shard_map/ppermute | solution.py:333
  32.2 0.0 collective-permute-done.6.left
  32.3 0.0 collective-permute-done.7.right
  32.3 0.0 collective-permute-done.8.across
  32.3 0.0 copy-start
  32.3 1.6 %copy-done = f32[512,1024]{1,0:T(8,128)S(1)} copy-done((f32[512,1024]{1,0:T(8,128)S(1)}, f32[512,1024]{1,0:T(8,128)}, u32[]{:S(2)}) %copy-start) | copy-done | bytes 2097176
  33.9 2.3 %shard_map.40 = (bf16[2,256,256]{2,1,0:T(8,128)(2,1)S(1)}, bf16[2,256,256]{2,1,0:T(8,128)(2,1)S(1)}, f32[128,1024]{1,0:T(8,128)S(1)}, f32[128,1024]{1,0:T(8,128)S(1)}, f32[2,128,128]{2,1,0:T(8,128)S(1)}) custom-call(f32[32,1536]{1,0:T(8,128)S(1)} %pad_maximum_fusion.1.own, f32[32,1536]{1,0:T(8,128)S(1)} %collective-permute-done.6.left, ...), custom_call_target="tpu_custom_call" | custom-call | flops 402653184 | bytes 4194304 | tf_op jit(solution)/shard_map/pallas_call | solution.py:320
  36.1 6.5 %collective-permute-start.10 = (f32[128,1024]{1,0:T(8,128)S(1)}, f32[128,1024]{1,0:T(8,128)S(1)}, u32[]{:S(2)}, u32[]{:S(2)}) collective-permute-start(f32[128,1024]{1,0:T(8,128)S(1)} %get-tuple-element.39.core1), channel_id=1, source_target_pairs={{0,8},{8,0},{16,24},{24,16},{32,40},{40,32},{48,56},{56,48},{64,72... | collective-permute-start | bytes 1572872 | tf_op jit(solution)/shard_map/ppermute | solution.py:373
  42.6 2.3 %collective-permute-start.9 = (f32[128,1024]{1,0:T(8,128)S(1)}, f32[128,1024]{1,0:T(8,128)S(1)}, u32[]{:S(2)}, u32[]{:S(2)}) collective-permute-start(f32[128,1024]{1,0:T(8,128)S(1)} %get-tuple-element.38.chip1), channel_id=1, source_target_pairs={{8,16},{16,8},{24,32},{32,24},{40,48},{48,40},{56,64},{64,56},{72,... | collective-permute-start | bytes 1572872 | tf_op jit(solution)/shard_map/ppermute | solution.py:370
  44.9 0.0 collective-permute-done.1
  45.0 3.0 %collective-permute-start.2 = (f32[32,3328]{1,0:T(8,128)S(1)}, f32[32,3328]{1,0:T(8,128)S(1)}, u32[]{:S(2)}, u32[]{:S(2)}) collective-permute-start(f32[32,3328]{1,0:T(8,128)S(1)} %pad_maximum_fusion.own), channel_id=1, source_target_pairs={{0,1},{1,0},{2,3},{3,2},{4,5},{5,4},{6,7},{7,6},{8,9},{9,8},{10,11... | collective-permute-start | bytes 1277960 | tf_op jit(solution)/shard_map/ppermute | solution.py:338
  48.0 3.7 %collective-permute-start.3 = (f32[32,3328]{1,0:T(8,128)S(1)}, f32[32,3328]{1,0:T(8,128)S(1)}, u32[]{:S(2)}, u32[]{:S(2)}) collective-permute-start(f32[32,3328]{1,0:T(8,128)S(1)} %pad_maximum_fusion.own), channel_id=1, source_target_pairs={{0,3},{1,2},{2,1},{3,0},{4,7},{5,6},{6,5},{7,4},{8,11},{9,10},{10,... | collective-permute-start | bytes 1277960 | tf_op jit(solution)/shard_map/ppermute | solution.py:338
  51.7 2.6 %collective-permute-start.4 = (f32[32,3328]{1,0:T(8,128)S(1)}, f32[32,3328]{1,0:T(8,128)S(1)}, u32[]{:S(2)}, u32[]{:S(2)}) collective-permute-start(f32[32,3328]{1,0:T(8,128)S(1)} %pad_maximum_fusion.own), channel_id=1, source_target_pairs={{0,2},{1,3},{2,0},{3,1},{4,6},{5,7},{6,4},{7,5},{8,10},{9,11},{10,... | collective-permute-start | bytes 1277960 | tf_op jit(solution)/shard_map/ppermute | solution.py:338
  54.2 2.4 %shard_map.41 = (f32[512,1024]{1,0:T(8,128)S(1)}, f32[128,128]{1,0:T(8,128)S(1)}) custom-call(f32[32,1536]{1,0:T(8,128)S(1)} %pad_maximum_fusion.1.own, f32[32,1536]{1,0:T(8,128)S(1)} %collective-permute-done.6.left, f32[32,1536]{1,0:T(8,128)S(1)} %collective-permute-done.7.right, f32[32,1536]{1,0:T(8,128)S(1)} %collective-permute-done.8.across, ...), custom_call_target="tpu_custom_call" | custom-call | flops 1207959552 | bytes 4194304 | tf_op jit(solution)/shard_map/pallas_call | solution.py:320
  56.7 0.5 collective-permute-done.2.left
  57.2 13.0 %collective-permute-done.3.right = f32[32,3328]{1,0:T(8,128)S(1)} collective-permute-done((f32[32,3328]{1,0:T(8,128)S(1)}, f32[32,3328]{1,0:T(8,128)S(1)}, u32[]{:S(2)}, u32[]{:S(2)}) %collective-permute-start.3) | collective-permute-done | bytes 426016 | tf_op jit(solution)/shard_map/ppermute | solution.py:338
  70.2 0.0 collective-permute-done.4.across
  70.2 2.3 %shard_map.42 = (bf16[2,256,256]{2,1,0:T(8,128)(2,1)S(1)}, bf16[2,256,256]{2,1,0:T(8,128)(2,1)S(1)}, bf16[2,128,128]{2,1,0:T(8,128)(2,1)S(1)}, bf16[2,128,128]{2...) custom-call(f32[2,128,128]{2,1,0:T(8,128)S(1)} %get-tuple-element.32.nxt_t.prev, ...), custom_call_target="tpu_custom_call" | custom-call | flops 402653184 | bytes 4194304 | tf_op jit(solution)/shard_map/pallas_call | solution.py:320
  72.5 0.0 collective-permute-done.10.got_core1
  72.6 0.0 collective-permute-done.9.got1
  72.6 2.2 %shard_map.43.u_in = f32[512,1024]{1,0:T(8,128)S(1)} custom-call(f32[128,1024]{1,0:T(8,128)S(1)} %get-tuple-element.38.chip1, f32[128,1024]{1,0:T(8,128)S(1)} %collective-permute-done.9.got1, f32[128,1024]{1,0:T(8,128)S(1)} %get-tuple-element.39.core1, f32[128,1024]{1,0:T(8,128)S(1)} %collective-permute-done.10.got_core1, ...), custom_call_target="tpu_custom_call" | custom-call | flops 1006632960 | bytes 4194304 | tf_op jit(solution)/shard_map/pallas_call | solution.py:320
  74.8 3.2 %shard_map.44 = (f32[512,1024]{1,0:T(8,128)S(1)}, bf16[2,256,256]{2,1,0:T(8,128)(2,1)S(1)}, bf16[2,256,256]{2,1,0:T(8,128)(2,1)S(1)}, bf16[2,128,128]{2,1,0:T(8,...) custom-call(f32[32,3328]{1,0:T(8,128)S(1)} %pad_maximum_fusion.own, ...), custom_call_target="tpu_custom_call" | custom-call | flops 1006632960 | bytes 4194304 | tf_op jit(solution)/shard_map/pallas_call | solution.py:320
  78.1 4.1 %collective-permute-start.12 = (f32[304,1024]{1,0:T(8,128)S(1)}, f32[304,1024]{1,0:T(8,128)S(1)}, u32[]{:S(2)}, u32[]{:S(2)}) collective-permute-start(f32[304,1024]{1,0:T(8,128)S(1)} %get-tuple-element.46.core35), channel_id=1, source_target_pairs={{0,8},{8,0},{16,24},{24,16},{32,40},{40,32},{48,56},{56,48},{64,72... | collective-permute-start | bytes 3735560 | tf_op jit(solution)/shard_map/ppermute | solution.py:373
  82.2 3.1 %collective-permute-start.13 = (f32[160,1024]{1,0:T(8,128)S(1)}, f32[160,1024]{1,0:T(8,128)S(1)}, u32[]{:S(2)}, u32[]{:S(2)}) collective-permute-start(f32[160,1024]{1,0:T(8,128)S(1)} %get-tuple-element.47.chip3), channel_id=1, source_target_pairs={{8,16},{16,8},{24,32},{32,24},{40,48},{48,40},{56,64},{64,56},{72,... | collective-permute-start | bytes 1966088 | tf_op jit(solution)/shard_map/ppermute | solution.py:370
  85.3 4.6 %collective-permute-start.11 = (f32[144,1024]{1,0:T(8,128)S(1)}, f32[144,1024]{1,0:T(8,128)S(1)}, u32[]{:S(2)}, u32[]{:S(2)}) collective-permute-start(f32[144,1024]{1,0:T(8,128)S(1)} %get-tuple-element.45.chip5), channel_id=1, source_target_pairs={{8,16},{16,8},{24,32},{32,24},{40,48},{48,40},{56,64},{64,56},{72,... | collective-permute-start | bytes 1769480 | tf_op jit(solution)/shard_map/ppermute | solution.py:370
  89.9 6.3 %collective-permute-done.13.got3 = f32[160,1024]{1,0:T(8,128)S(1)} collective-permute-done((f32[160,1024]{1,0:T(8,128)S(1)}, f32[160,1024]{1,0:T(8,128)S(1)}, u32[]{:S(2)}, u32[]{:S(2)}) %collective-permute-start.13) | collective-permute-done | bytes 655392 | tf_op jit(solution)/shard_map/ppermute | solution.py:370
  96.2 0.0 collective-permute-done.12.got_core35
  96.2 2.8 %shard_map.45 = (f32[512,1024]{1,0:T(8,128)S(1)}, f32[2,128,1024]{2,1,0:T(8,128)S(1)}) custom-call(f32[128,1024]{1,0:T(8,128)S(1)} %get-tuple-element.38.chip1, f32[128,1024]{1,0:T(8,128)S(1)} %collective-permute-done.9.got1, f32[128,1024]{1,0:T(8,128)S(1)} %get-tuple-element.39.core1, f32[128,1024]{1,0:T(8,128)S(1)} %collective-permute-done.10.got_core1, ...), custom_call_target="tpu_custom_call" | custom-call | flops 1207959552 | bytes 4194304 | tf_op jit(solution)/shard_map/pallas_call | solution.py:320
  99.0 2.1 %shard_map.46 = (f32[512,1024]{1,0:T(8,128)}, bf16[2,128,128]{2,1,0:T(8,128)(2,1)S(1)}, bf16[2,128,128]{2,1,0:T(8,128)(2,1)S(1)}) custom-call(f32[32,3328]{1,0:T(8,128)S(1)} %pad_maximum_fusion.own, f32[32,3328]{1,0:T(8,128)S(1)} %collective-permute-done.2.left, f32[32,3328]{1,0:T(8,128)S(1)} %collective-permute-done.3.right, ...), custom_call_target="tpu_custom_call" | custom-call | flops 503316480 | bytes 4194304 | tf_op jit(solution)/shard_map/pallas_call | solution.py:320
  101.1 1.5 %collective-permute-done.11.got5 = f32[144,1024]{1,0:T(8,128)S(1)} collective-permute-done((f32[144,1024]{1,0:T(8,128)S(1)}, f32[144,1024]{1,0:T(8,128)S(1)}, u32[]{:S(2)}, u32[]{:S(2)}) %collective-permute-start.11) | collective-permute-done | bytes 589856 | tf_op jit(solution)/shard_map/ppermute | solution.py:370
  102.5 2.3 %shard_map.47 = f32[512,1024]{1,0:T(8,128)} custom-call(f32[144,1024]{1,0:T(8,128)S(1)} %get-tuple-element.45.chip5, f32[144,1024]{1,0:T(8,128)S(1)} %collective-permute-done.11.got5, f32[304,1024]{1,0:T(8,128)S(1)} %get-tuple-element.46.core35, f32[304,1024]{1,0:T(8,128)S(1)} %collective-permute-done.12.got_core35, ...), custom_call_target="tpu_custom_call", output_to_operand_aliasing={{}: (8, {})} | custom-call | flops 402653184 | tf_op jit(solution)/shard_map/pallas_call | solution.py:320
  (5 shorter events, 0.1 us)
Async XLA Ops:
  0.0 0.9 copy-start.1
  0.9 0.9 copy-start.2
  1.8 13.8 %collective-permute-start.5 = (f32[16,1536]{1,0:T(8,128)S(1)}, f32[16,1536]{1,0:T(8,128)S(1)}, u32[]{:S(2)}, u32[]{:S(2)}) collective-permute-start(f32[16,1536]{1,0:T(8,128)S(1)} %shard_map.39), channel_id=1, source_target_pairs={{0,4},{1,5},{2,6},{3,7},{4,0},{5,1},{6,2},{7,3},{8,12},{9,13},{10,... | collective-permute-start | bytes 294920 | tf_op jit(solution)/shard_map/ppermute | solution.py:333
  12.5 12.6 %collective-permute-start = (f32[16,1024]{1,0:T(8,128)S(1)}, f32[16,1024]{1,0:T(8,128)S(1)}, u32[]{:S(2)}, u32[]{:S(2)}) collective-permute-start(f32[16,1024]{1,0:T(8,128)S(1)} %shard_map.37), channel_id=1, source_target_pairs={{0,8},{8,16},{16,24},{24,32},{32,40},{40,48},{48,56},{56,64},{64,7... | collective-permute-start | bytes 196616 | tf_op jit(solution)/shard_map/ppermute | solution.py:348
  15.7 16.6 %collective-permute-start.6 = (f32[32,1536]{1,0:T(8,128)S(1)}, f32[32,1536]{1,0:T(8,128)S(1)}, u32[]{:S(2)}, u32[]{:S(2)}) collective-permute-start(f32[32,1536]{1,0:T(8,128)S(1)} %pad_maximum_fusion.1.own), channel_id=1, source_target_pairs={{0,1},{1,0},{2,3},{3,2},{4,5},{5,4},{6,7},{7,6},{8,9},{9,8},{10,11... | collective-permute-start | bytes 589832 | tf_op jit(solution)/shard_map/ppermute | solution.py:338
  18.8 13.5 %collective-permute-start.7 = (f32[32,1536]{1,0:T(8,128)S(1)}, f32[32,1536]{1,0:T(8,128)S(1)}, u32[]{:S(2)}, u32[]{:S(2)}) collective-permute-start(f32[32,1536]{1,0:T(8,128)S(1)} %pad_maximum_fusion.1.own), channel_id=1, source_target_pairs={{0,3},{1,2},{2,1},{3,0},{4,7},{5,6},{6,5},{7,4},{8,11},{9,10},{10,... | collective-permute-start | bytes 589832 | tf_op jit(solution)/shard_map/ppermute | solution.py:338
  22.5 9.7 %collective-permute-start.8 = (f32[32,1536]{1,0:T(8,128)S(1)}, f32[32,1536]{1,0:T(8,128)S(1)}, u32[]{:S(2)}, u32[]{:S(2)}) collective-permute-start(f32[32,1536]{1,0:T(8,128)S(1)} %pad_maximum_fusion.1.own), channel_id=1, source_target_pairs={{0,2},{1,3},{2,0},{3,1},{4,6},{5,7},{6,4},{7,5},{8,10},{9,11},{10,... | collective-permute-start | bytes 589832 | tf_op jit(solution)/shard_map/ppermute | solution.py:338
  25.1 0.9 copy-start.3
  26.1 18.9 %collective-permute-start.1 = (f32[16,3328]{1,0:T(8,128)S(1)}, f32[16,3328]{1,0:T(8,128)S(1)}, u32[]{:S(2)}, u32[]{:S(2)}) collective-permute-start(f32[16,3328]{1,0:T(8,128)S(1)} %shard_map.38), channel_id=1, source_target_pairs={{0,4},{1,5},{2,6},{3,7},{4,0},{5,1},{6,2},{7,3},{8,12},{9,13},{10,... | collective-permute-start | bytes 638984 | tf_op jit(solution)/shard_map/ppermute | solution.py:333
  32.3 1.6 %copy-start = (f32[512,1024]{1,0:T(8,128)S(1)}, f32[512,1024]{1,0:T(8,128)}, u32[]{:S(2)}) copy-start(f32[512,1024]{1,0:T(8,128)} %x.3) | copy-start | bytes 6291460
  36.1 36.4 %collective-permute-start.10 = (f32[128,1024]{1,0:T(8,128)S(1)}, f32[128,1024]{1,0:T(8,128)S(1)}, u32[]{:S(2)}, u32[]{:S(2)}) collective-permute-start(f32[128,1024]{1,0:T(8,128)S(1)} %get-tuple-element.39.core1), channel_id=1, source_target_pairs={{0,8},{8,0},{16,24},{24,16},{32,40},{40,32},{48,56},{56,48},{64,72... | collective-permute-start | bytes 1572872 | tf_op jit(solution)/shard_map/ppermute | solution.py:373
  42.6 29.9 %collective-permute-start.9 = (f32[128,1024]{1,0:T(8,128)S(1)}, f32[128,1024]{1,0:T(8,128)S(1)}, u32[]{:S(2)}, u32[]{:S(2)}) collective-permute-start(f32[128,1024]{1,0:T(8,128)S(1)} %get-tuple-element.38.chip1), channel_id=1, source_target_pairs={{8,16},{16,8},{24,32},{32,24},{40,48},{48,40},{56,64},{64,56},{72,... | collective-permute-start | bytes 1572872 | tf_op jit(solution)/shard_map/ppermute | solution.py:370
  45.0 12.2 %collective-permute-start.2 = (f32[32,3328]{1,0:T(8,128)S(1)}, f32[32,3328]{1,0:T(8,128)S(1)}, u32[]{:S(2)}, u32[]{:S(2)}) collective-permute-start(f32[32,3328]{1,0:T(8,128)S(1)} %pad_maximum_fusion.own), channel_id=1, source_target_pairs={{0,1},{1,0},{2,3},{3,2},{4,5},{5,4},{6,7},{7,6},{8,9},{9,8},{10,11... | collective-permute-start | bytes 1277960 | tf_op jit(solution)/shard_map/ppermute | solution.py:338
  48.0 22.2 %collective-permute-start.3 = (f32[32,3328]{1,0:T(8,128)S(1)}, f32[32,3328]{1,0:T(8,128)S(1)}, u32[]{:S(2)}, u32[]{:S(2)}) collective-permute-start(f32[32,3328]{1,0:T(8,128)S(1)} %pad_maximum_fusion.own), channel_id=1, source_target_pairs={{0,3},{1,2},{2,1},{3,0},{4,7},{5,6},{6,5},{7,4},{8,11},{9,10},{10,... | collective-permute-start | bytes 1277960 | tf_op jit(solution)/shard_map/ppermute | solution.py:338
  51.7 18.5 %collective-permute-start.4 = (f32[32,3328]{1,0:T(8,128)S(1)}, f32[32,3328]{1,0:T(8,128)S(1)}, u32[]{:S(2)}, u32[]{:S(2)}) collective-permute-start(f32[32,3328]{1,0:T(8,128)S(1)} %pad_maximum_fusion.own), channel_id=1, source_target_pairs={{0,2},{1,3},{2,0},{3,1},{4,6},{5,7},{6,4},{7,5},{8,10},{9,11},{10,... | collective-permute-start | bytes 1277960 | tf_op jit(solution)/shard_map/ppermute | solution.py:338
  78.1 18.2 %collective-permute-start.12 = (f32[304,1024]{1,0:T(8,128)S(1)}, f32[304,1024]{1,0:T(8,128)S(1)}, u32[]{:S(2)}, u32[]{:S(2)}) collective-permute-start(f32[304,1024]{1,0:T(8,128)S(1)} %get-tuple-element.46.core35), channel_id=1, source_target_pairs={{0,8},{8,0},{16,24},{24,16},{32,40},{40,32},{48,56},{56,48},{64,72... | collective-permute-start | bytes 3735560 | tf_op jit(solution)/shard_map/ppermute | solution.py:373
  82.2 14.0 %collective-permute-start.13 = (f32[160,1024]{1,0:T(8,128)S(1)}, f32[160,1024]{1,0:T(8,128)S(1)}, u32[]{:S(2)}, u32[]{:S(2)}) collective-permute-start(f32[160,1024]{1,0:T(8,128)S(1)} %get-tuple-element.47.chip3), channel_id=1, source_target_pairs={{8,16},{16,8},{24,32},{32,24},{40,48},{48,40},{56,64},{64,56},{72,... | collective-permute-start | bytes 1966088 | tf_op jit(solution)/shard_map/ppermute | solution.py:370
  85.3 17.2 %collective-permute-start.11 = (f32[144,1024]{1,0:T(8,128)S(1)}, f32[144,1024]{1,0:T(8,128)S(1)}, u32[]{:S(2)}, u32[]{:S(2)}) collective-permute-start(f32[144,1024]{1,0:T(8,128)S(1)} %get-tuple-element.45.chip5), channel_id=1, source_target_pairs={{8,16},{16,8},{24,32},{32,24},{40,48},{48,40},{56,64},{64,56},{72,... | collective-permute-start | bytes 1769480 | tf_op jit(solution)/shard_map/ppermute | solution.py:370

commit v3 on v2

--- a/solution.py
+++ b/solution.py
@@ -10,6 +10,8 @@
 F32 = jnp.float32
 BF16 = jnp.bfloat16
 SPAN = 512
+WIDE = 1024
+EARLY = 2
 XS = 4
 SHIFTED = ((1, 1), (2, 1), (3, 0), (3, 1), (4, 0), (4, 1), (5, 0), (5, 1))
 
@@ -24,7 +26,7 @@
 
 
 def dot3(a, b):
-    return mm(a[0], b[0]) + (mm(a[0], b[1]) + mm(a[1], b[0]))
+    return mm(jnp.concatenate([a[0], a[0], a[1]], axis=1), jnp.concatenate([b[0], b[1], b[0]], axis=0))
 
 
 def product(a, b):
@@ -71,11 +73,8 @@
 
 
 def spans(body, width):
-    def step(c, carry):
-        body(pl.ds(pl.multiple_of(c * SPAN, SPAN), SPAN))
-        return carry
-
-    lax.fori_loop(0, width // SPAN, step, 0)
+    for start in range(0, width, WIDE):
+        body(slice(start, start + WIDE))
 
 
 def lay(out, *parts):
@@ -85,6 +84,10 @@
         at += part.shape[1]
 
 
+def halves(turned):
+    return [turned[2, :, 0:256], turned[2, :, 256:512]]
+
+
 def ends(turned, r):
     return turned[r, :, 0:128], turned[r, :, 384:512]
 
@@ -97,7 +100,7 @@
     lay(
         out,
         turned[0], *ends(turned, 1), factors[0, 0], factors[0, 1],
-        turned[1, :, 128:384], factors[1, 0], factors[1, 1],
+        turned[1, :, 128:384], factors[1, 0], factors[1, 1], *halves(turned)[:EARLY],
     )
 
 
@@ -107,7 +110,7 @@
         out,
         came[0], came[1], factors[2, 0], *ends(turned, 3),
         turned[3, :, 128:384], came[3], factors[3, 0], came[2], turned[4], came[4], came[5], *ends(turned, 5),
-        turned[5, :, 128:384], came[6], came[7], turned[2],
+        turned[5, :, 128:384], came[6], came[7], *halves(turned)[EARLY:],
     )
 
 
@@ -161,13 +164,13 @@
     return jnp.where(odd, values[1], values[0]), jnp.where(odd, values[0], values[1])
 
 
-def spread_and_ahead(basis, buf, at, nxt_t, spread, chip, core, core_at, ph, pl_, uh, ul, lh, ll):
+def spread_and_ahead(bases, buf, at, nxt_t, spread, chip, core, core_at, ph, pl_, uh, ul, lh, ll):
     tops = []
     for side in range(2):
         put((uh, ul), side, spread[side])
         nxt = block(buf, at + 256 + side * NB, NB)
         nxt_t[side] = nxt
-        matrix = group_matrix(block(basis, side * 256, 256), block(buf, at + side * NB, NB))
+        matrix = group_matrix(bases[side], block(buf, at + side * NB, NB))
         put((ph, pl_), side, matrix)
         look = look_ahead(side, nxt, matrix)
         put((lh, ll), side, look)
@@ -177,10 +180,15 @@
     core[core_at + NB : core_at + NB + 16, :] = second
 
 
-def ahead_kernel(prev_t, prev_tail, u, own, left, right, across, *rest):
-    ph, pl_, uh, ul, chip, core, nxt_t, basis, buf, last_block, lh, ll = rest
-    parts = (own, left, right, across)
-    assemble(parts, basis, 2816)
+def ahead_kernel(prev_t, prev_tail, u, *rest):
+    early, parts = rest[:4], rest[4:8]
+    ph, pl_, uh, ul, chip, core, nxt_t, first_basis, second_basis, buf, last_block, lh, ll = rest[8:]
+    bases = (first_basis, second_basis)
+    for side, basis in enumerate(bases):
+        if side < EARLY:
+            assemble(early, basis, 1536 + 256 * side)
+        else:
+            assemble(parts, basis, 2816 + 256 * (side - EARLY))
     assemble(parts, buf)
     assemble(parts, last_block, 2816 - NB)
     odd = place()[2] == 1
@@ -188,7 +196,7 @@
         chip[NB + 16 :, k * NB : (k + 1) * NB] = last_block[k]
         core[NB + 16 :, k * NB : (k + 1) * NB] = last_block[k]
     spread = (product(prev_t[0].T, block(buf, 0, NB)), prev_tail[...])
-    spread_and_ahead(basis, buf, NB, nxt_t, spread, chip, core, 0, ph, pl_, uh, ul, lh, ll)
+    spread_and_ahead([block(b, 0, 256) for b in bases], buf, NB, nxt_t, spread, chip, core, 0, ph, pl_, uh, ul, lh, ll)
 
     def body(cols):
         heads = [dot3(get((lh, ll), side), split(u[side * 256 : side * 256 + 256, cols])) for side in range(2)]
@@ -197,7 +205,9 @@
     spans(body, u.shape[1])
 
 
-def middle_kernel(own, left, right, across, prev_t, u_in, prev_core, *rest):
+def middle_kernel(
+    chip1, got1, core1, got_core1, uh1, ul1, ph2, pl2, own, left, right, across, prev_t, u_in, prev_core, *rest
+):
     u, ph, pl_, uh, ul, chip, core, nxt_t, buf, basis, tips, mh, ml, lh, ll = rest
     parts = (own, left, right, across)
     assemble(parts, buf, 640)
@@ -207,14 +217,16 @@
     start = prev_core.shape[0]
     put((mh, ml), slice(None), group_matrix(block(buf, 0, 256), block(buf, 256, NB)))
     spread = (product(prev_t[0].T, block(buf, 512, NB)), product(prev_t[1].T, block(buf, 384, NB)))
-    spread_and_ahead(basis, tips, 0, nxt_t, spread, chip, core, start, ph, pl_, uh, ul, lh, ll)
+    spread_and_ahead([block(basis, 256 * k, 256) for k in range(2)], tips, 0, nxt_t, spread, chip, core, start, ph, pl_, uh, ul, lh, ll)
 
     def body(cols):
         core[:start, cols] = prev_core[:, cols]
-        panel = u_in[128:384, cols]
+        totals = both_sides(chip1, got1, core1, got_core1, 0, STRIP, cols)
+        upper, lower = straddle_and_even(totals, uh1, ul1, ph2, pl2, u_in, cols)
+        panel = jnp.concatenate([upper[NB:], lower[:NB]], axis=0)
         panel = panel - dot3((mh[...], ml[...]), split(panel))
+        top, bottom = upper[:NB], lower[NB:]
         u[128:384, cols] = panel
-        top, bottom = u_in[0:128, cols], u_in[384:512, cols]
         u[0:128, cols] = top
         u[384:512, cols] = bottom
         heads = [
@@ -240,26 +252,28 @@
 EVERY = slice(None)
 
 
-def even_kernel(chip1, got1, core1, got_core1, uh, ul, ph, pl_, u_in, u):
-    def body(cols):
-        totals = both_sides(chip1, got1, core1, got_core1, 0, STRIP, cols)
-        straddle_and_even(totals, uh, ul, ph, pl_, u_in, u, cols)
-
-    spans(body, u.shape[1])
-
-
-def straddle_and_even(totals, uh, ul, ph, pl_, u_in, u, cols):
+def straddle_and_even(totals, uh, ul, ph, pl_, u_in, cols):
+    halves = []
     for side in range(2):
         near = slice(0, 128) if side == 0 else slice(384, 512)
         far = slice(128, 256) if side == 0 else slice(256, 384)
         panel = u_in[near, cols] - dot3((uh[side], ul[side]), split(totals[side]))
         pair = [panel, u_in[far, cols]] if side == 0 else [u_in[far, cols], panel]
         both = jnp.concatenate(pair, axis=0)
-        u[side * 256 : side * 256 + 256, cols] = both - dot3((ph[side], pl_[side]), split(both))
-
-
-def late_even_kernel(chip1, got1, core1, got_core1, chip3, got3, core35, got_core35, uh, ul, ph, pl_, u_in, *rest):
-    u, sums, qh, ql = rest
+        halves.append(both - dot3((ph[side], pl_[side]), split(both)))
+    return halves
+
+
+def operators_kernel(own, left, right, across, prev_t, mh, ml, uh, ul, buf):
+    assemble((own, left, right, across), buf, 2304)
+    put((mh, ml), slice(None), group_matrix(block(buf, 0, 256), block(buf, 256, NB)))
+    put((uh, ul), slice(None), product(prev_t[1].T, block(buf, 384, NB)))
+
+
+def final_middle_kernel(
+    chip1, got1, core1, got_core1, chip3, got3, core35, got_core35, uh3, ul3, ph, pl_, mh, ml, th, tl, prev_t, u_in, *rest
+):
+    strips, center, sums, uh, ul, qh, ql = rest
     three = (chip3, got3, core35, got_core35)
     for side, value in enumerate(both_sides(*three, 0, OPERATOR, EVERY)):
         put((qh, ql), side, unpacked(value))
@@ -270,51 +284,42 @@
         totals = [threes[side] - dot3(get((qh, ql), side), split(ones[side])) for side in range(2)]
         for side in range(2):
             sums[side, :, cols] = totals[side]
-        straddle_and_even(totals, uh, ul, ph, pl_, u_in, u, cols)
-
-    spans(body, u.shape[1])
-
-
-def final_middle_kernel(own, left, right, across, prev_t, u_in, got3, got_core35, *rest):
-    out, uh, ul, buf, mh, ml, rows, sem = rest
-    assemble((own, left, right, across), buf, 2304)
-    put((mh, ml), slice(None), group_matrix(block(buf, 0, 256), block(buf, 256, NB)))
-    copies = []
-    for c in range(u_in.shape[1] // SPAN):
-        cols = slice(c * SPAN, c * SPAN + SPAN)
-        panel = u_in[128:384, cols]
-        rows[c] = panel - dot3((mh[...], ml[...]), split(panel))
-        copies.append(pltpu.make_async_copy(rows.at[c], out.at[128:384, cols], sem.at[c]))
-        copies[-1].start()
+        upper, lower = straddle_and_even(totals, uh3, ul3, ph, pl_, u_in, cols)
+        strips[0, :, cols] = upper[:NB]
+        strips[1, :, cols] = lower[NB:]
+        panel = jnp.concatenate([upper[NB:], lower[:NB]], axis=0)
+        center[:, cols] = panel - dot3((mh[...], ml[...]), split(panel))
+
+    spans(body, u_in.shape[1])
     head = unpacked(jnp.where(place()[2] == 1, got_core35[BLOCK, :], got3[BLOCK, :]))
     put((uh, ul), 0, product(prev_t[0].T, head))
-    put((uh, ul), 1, product(prev_t[1].T, block(buf, 384, NB)))
-    for copy in copies:
-        copy.wait()
-
-
-def last_kernel(chip5, got5, core35, got_core35, sums, uh, ul, u_in, held_out, out, qh, ql, rows, sem):
-    del held_out
+    uh[1] = th[...]
+    ul[1] = tl[...]
+
+
+def last_kernel(chip5, got5, core35, got_core35, sums, uh, ul, strips, center, out, qh, ql, rows, sem):
+    count = 2 * sums.shape[2] // SPAN
+    copies = [pltpu.make_async_copy(center, out.at[128:384, :], sem.at[count])]
+    copies[0].start()
     start = core35.shape[0] - chip5.shape[0]
     five = (chip5, got5, core35, got_core35)
     for side, value in enumerate(both_sides(*five, start, OPERATOR, EVERY)):
         put((qh, ql), side, unpacked(value))
-    copies = []
-    for c in range(u_in.shape[1] // SPAN):
+    for c in range(sums.shape[2] // SPAN):
         cols = slice(c * SPAN, c * SPAN + SPAN)
         fives = both_sides(*five, start, STRIP, cols)
         for side in range(2):
             near = slice(0, 128) if side == 0 else slice(384, 512)
             k = 2 * c + side
             total = fives[side] - dot3(get((qh, ql), side), split(sums[side, :, cols]))
-            rows[k] = u_in[near, cols] - dot3((uh[side], ul[side]), split(total))
+            rows[k] = strips[side, :, cols] - dot3((uh[side], ul[side]), split(total))
             copies.append(pltpu.make_async_copy(rows.at[k], out.at[near, cols], sem.at[k]))
             copies[-1].start()
     for copy in copies:
         copy.wait()
 
 
-def call(kernel, outs, scratch, flops, *args, far=(), far_out=(), sems=0, aliases={}):
+def call(kernel, outs, scratch, flops, *args, far=(), far_out=(), sems=0):
     vmem = pl.BlockSpec(memory_space=pltpu.VMEM)
     hbm = pl.BlockSpec(memory_space=pltpu.HBM)
     return pl.pallas_call(
@@ -322,7 +327,6 @@
         out_shape=[jax.ShapeDtypeStruct(s, t) for s, t in outs],
         in_specs=[hbm if k in far else vmem for k in range(len(args))],
         out_specs=[hbm if k in far_out else vmem for k in range(len(outs))],
-        input_output_aliases=aliases,
         scratch_shapes=[pltpu.VMEM(s, t) for s, t in scratch] + [pltpu.SemaphoreType.DMA((sems,))] * bool(sems),
         cost_estimate=pl.CostEstimate(flops=flops, bytes_accessed=0 if far else 4 << 20, transcendentals=0),
         compiler_params=pltpu.CompilerParams(vmem_limit_bytes=24 << 20),
@@ -346,9 +350,9 @@
     turned = jnp.transpose(reflectors, (0, 2, 1))
     (shifted,) = call(shift_kernel, [((16, 1024), F32)], [], 1 << 20, factors)
     slid = lax.ppermute(shifted, "row", [(k, k + 1) for k in range(rows - 1)])
-    (a,) = call(first_payload_kernel, [((16, 1536), F32)], [], 1 << 20, turned, factors)
+    (a,) = call(first_payload_kernel, [((16, 1536 + 256 * EARLY), F32)], [], 1 << 20, turned, factors)
     a2 = far_half(a)
-    (b,) = call(rest_payload_kernel, [((16, 3328), F32)], [], 1 << 20, turned, factors, slid)
+    (b,) = call(rest_payload_kernel, [((16, 3328 - 256 * EARLY), F32)], [], 1 << 20, turned, factors, slid)
     b2 = far_half(b)
     a = near_parts(a, a2)
     b = near_parts(b, b2)
@@ -394,49 +398,39 @@
     ph, pl_, uh, ul, chip3, core3, nxt_t = call(
         ahead_kernel,
         [pair, pair, small, small, long, long, ends_t],
-        [held(512), held(640), held(NB), look, look],
+        [held(256), held(256), held(640), held(NB), look, look],
         4 * unit,
-        nxt_t, tail, u, *b,
+        nxt_t, tail, u, *a, *b,
     )
     got3 = across_chips(chip3)
-    (u,) = call(even_kernel, [whole], [], 10 * unit, *ones, uh, ul, ph, pl_, u)
     u, ph, pl_, uh, ul, chip5, core35, nxt_t = call(
         middle_kernel,
         [whole, pair, pair, small, small, shorter, double, ends_t],
         [held(640), held(512), held(512), mid, mid, look, look],
-        10 * unit,
-        *b, nxt_t, u, core3,
+        20 * unit,
+        *ones, uh, ul, ph, pl_, *b, nxt_t, u, core3,
     )
     got5 = across_chips(chip5)
     got_core35 = across_cores(core35)
-    u, sums = call(
-        late_even_kernel,
-        [whole, strips],
+    single = ((NB, NB), BF16)
+    mh, ml, th, tl = call(operators_kernel, [mid, mid, single, single], [held(512)], unit, *b, nxt_t)
+    tops, center, sums, uh, ul = call(
+        final_middle_kernel,
+        [strips, ((2 * NB, width), F32), strips, small, small],
         [small, small],
-        12 * unit,
-        *ones, chip3, got3, core35, got_core35, uh, ul, ph, pl_, u,
-    )
-    out, uh, ul = call(
-        final_middle_kernel,
-        [whole, small, small],
-        [held(512), mid, mid, ((width // SPAN, 2 * NB, SPAN), F32)],
-        5 * unit,
-        *b, nxt_t, u, got3, got_core35,
-        far_out=(0,),
-        sems=width // SPAN,
-    )
-    (out,) = call(
+        20 * unit,
+        *ones, chip3, got3, core35, got_core35, uh, ul, ph, pl_, mh, ml, th, tl, nxt_t, u,
+    )
+    (vectors,) = call(
         last_kernel,
         [whole],
         [small, small, ((2 * width // SPAN, NB, SPAN), F32)],
         4 * unit,
-        chip5, got5, core35, got_core35, sums, uh, ul, u, out,
-        far=(8,),
+        chip5, got5, core35, got_core35, sums, uh, ul, tops, center,
         far_out=(0,),
-        sems=2 * width // SPAN,
-        aliases={8: 0},
-    )
-    return out
+        sems=2 * width // SPAN + 1,
+    )
+    return vectors
 
 
 def solution(mesh):

time: 105 us -> 107 us (1.019)
  the two profiles are of different devices: /device:TPU:57 before, /device:TPU:25 now
where the time goes in v3:
time: 107 us; the launch traced here: 106 us
  starting transfers between devices  63 us (59%)
  waiting for transfers between devices  23.9 us (22%)
  Pallas kernels  14.5 us (14%)
  local copies, waits for them, and re-layouts  4.33 us (4%)
    ppermute x2, starting transfers between devices, far_half(): return lax.ppermute(payload, 'vec', [(v, v ^ XS) for v in range(2 * XS)])  20.6 us
    ppermute x6, starting transfers between devices, near_parts(): lax.ppermute(both, 'vec', [(v, v ^ step) for v in range(2 * XS)])  18.6 us
    pallas_call x10, Pallas kernels, call(): pl.pallas_call(kernel, out_shape=[jax.ShapeDtypeStruct(s, t) for s, t in...  14.5 us
    ppermute x3, starting transfers between devices, across_chips(): return lax.ppermute(value, 'row', chip_pairs)  12.7 us
    ppermute x6, waiting for transfers between devices, near_parts(): lax.ppermute(both, 'vec', [(v, v ^ step) for v in range(2 * XS)])  9.94 us
    ppermute x3, waiting for transfers between devices, across_chips(): return lax.ppermute(value, 'row', chip_pairs)  9.46 us
    ppermute x1, starting transfers between devices, rounds(): slid = lax.ppermute(shifted, 'row', [(k, k + 1) for k in range(rows - 1)])  6.21 us
    ppermute x2, starting transfers between devices, across_cores(): return lax.ppermute(value, 'row', core_pairs)  4.82 us
  transfers between devices with their start and end apart: 14, of which 7 were waited for; matrix products, arithmetic and copies ran while one was open for 0% of the time, Pallas kernels for 8%

profile of v3, /device:TPU:25, one launch (start us, length us, event | category | flops | bytes accessed | tf_op | source)
XLA Modules:
  0.0 106.2 jit_solution(16194595079057173130)
XLA Ops:
  0.0 0.0 copy-start.1
  0.0 0.9 copy-done.1
  0.9 0.0 copy-start.2
  0.9 0.9 copy-done.2
  1.8 10.6 %collective-permute-start = (f32[16,2048]{1,0:T(8,128)S(1)}, f32[16,2048]{1,0:T(8,128)S(1)}, u32[]{:S(2)}, u32[]{:S(2)}) collective-permute-start(f32[16,2048]{1,0:T(8,128)S(1)} %shard_map.37), channel_id=1, source_target_pairs={{0,4},{1,5},{2,6},{3,7},{4,0},{5,1},{6,2},{7,3},{8,12},{9,13},{10,... | collective-permute-start | bytes 393224 | tf_op jit(solution)/shard_map/ppermute | solution.py:337
  12.5 3.2 %collective-permute-done = f32[16,2048]{1,0:T(8,128)S(1)} collective-permute-done((f32[16,2048]{1,0:T(8,128)S(1)}, f32[16,2048]{1,0:T(8,128)S(1)}, u32[]{:S(2)}, u32[]{:S(2)}) %collective-permute-start) | collective-permute-done | bytes 131104 | tf_op jit(solution)/shard_map/ppermute | solution.py:337
  15.7 3.1 %collective-permute-start.1 = (f32[32,2048]{1,0:T(8,128)S(1)}, f32[32,2048]{1,0:T(8,128)S(1)}, u32[]{:S(2)}, u32[]{:S(2)}) collective-permute-start(f32[32,2048]{1,0:T(8,128)S(1)} %pad_maximum_fusion.1.own.rest_0_), channel_id=1, source_target_pairs={{0,1},{1,0},{2,3},{3,2},{4,5},{5,4},{6,7},{7,6},{8,9},{9,8},{10,11... | collective-permute-start | bytes 786440 | tf_op jit(solution)/shard_map/ppermute | solution.py:342
  18.8 3.7 %collective-permute-start.2 = (f32[32,2048]{1,0:T(8,128)S(1)}, f32[32,2048]{1,0:T(8,128)S(1)}, u32[]{:S(2)}, u32[]{:S(2)}) collective-permute-start(f32[32,2048]{1,0:T(8,128)S(1)} %pad_maximum_fusion.1.own.rest_0_), channel_id=1, source_target_pairs={{0,3},{1,2},{2,1},{3,0},{4,7},{5,6},{6,5},{7,4},{8,11},{9,10},{10,... | collective-permute-start | bytes 786440 | tf_op jit(solution)/shard_map/ppermute | solution.py:342
  22.5 2.6 %collective-permute-start.3 = (f32[32,2048]{1,0:T(8,128)S(1)}, f32[32,2048]{1,0:T(8,128)S(1)}, u32[]{:S(2)}, u32[]{:S(2)}) collective-permute-start(f32[32,2048]{1,0:T(8,128)S(1)} %pad_maximum_fusion.1.own.rest_0_), channel_id=1, source_target_pairs={{0,2},{1,3},{2,0},{3,1},{4,6},{5,7},{6,4},{7,5},{8,10},{9,11},{10,... | collective-permute-start | bytes 786440 | tf_op jit(solution)/shard_map/ppermute | solution.py:342
  25.1 6.2 %collective-permute-start.6 = (f32[16,1024]{1,0:T(8,128)S(1)}, f32[16,1024]{1,0:T(8,128)S(1)}, u32[]{:S(2)}, u32[]{:S(2)}) collective-permute-start(f32[16,1024]{1,0:T(8,128)S(1)} %shard_map.40), channel_id=1, source_target_pairs={{0,8},{8,16},{16,24},{24,32},{32,40},{40,48},{48,56},{56,64},{64,7... | collective-permute-start | bytes 196616 | tf_op jit(solution)/shard_map/ppermute | solution.py:352
  31.3 1.3 %collective-permute-done.6.slid = f32[16,1024]{1,0:T(8,128)S(1)} collective-permute-done((f32[16,1024]{1,0:T(8,128)S(1)}, f32[16,1024]{1,0:T(8,128)S(1)}, u32[]{:S(2)}, u32[]{:S(2)}) %collective-permute-start.6) | collective-permute-done | bytes 65568 | tf_op jit(solution)/shard_map/ppermute | solution.py:352
  32.6 0.0 copy-start.3
  32.7 0.9 copy-done.3
  33.6 10.0 %collective-permute-start.7 = (f32[16,2816]{1,0:T(8,128)S(1)}, f32[16,2816]{1,0:T(8,128)S(1)}, u32[]{:S(2)}, u32[]{:S(2)}) collective-permute-start(f32[16,2816]{1,0:T(8,128)S(1)} %shard_map.41), channel_id=1, source_target_pairs={{0,4},{1,5},{2,6},{3,7},{4,0},{5,1},{6,2},{7,3},{8,12},{9,13},{10,... | collective-permute-start | bytes 540680 | tf_op jit(solution)/shard_map/ppermute | solution.py:337
  43.6 0.0 collective-permute-done.1.left.rest_1_
  43.6 0.0 collective-permute-done.2.right.rest_2_
  43.6 0.0 collective-permute-done.3.across.rest_3_
  43.6 0.0 copy-start
  43.6 1.6 %copy-done = f32[512,1024]{1,0:T(8,128)S(1)} copy-done((f32[512,1024]{1,0:T(8,128)S(1)}, f32[512,1024]{1,0:T(8,128)}, u32[]{:S(2)}) %copy-start) | copy-done | bytes 2097176
  45.2 1.7 %shard_map.38 = (bf16[2,256,256]{2,1,0:T(8,128)(2,1)S(1)}, bf16[2,256,256]{2,1,0:T(8,128)(2,1)S(1)}, f32[128,1024]{1,0:T(8,128)S(1)}, f32[128,1024]{1,0:T(8,128)S(1)}, f32[2,128,128]{2,1,0:T(8,128)S(1)}) custom-call(f32[32,2048]{1,0:T(8,128)S(1)} %pad_maximum_fusion.1.own.rest_0_, f32[32,2048]{1,0:T(8,128)S(1)} %collective-permute-done.1.left.rest_1_, ...), custom_call_target="tpu_custom_call" | custom-call | flops 402653184 | bytes 4194304 | tf_op jit(solution)/shard_map/pallas_call | solution.py:325
  46.9 5.8 %collective-permute-start.4 = (f32[128,1024]{1,0:T(8,128)S(1)}, f32[128,1024]{1,0:T(8,128)S(1)}, u32[]{:S(2)}, u32[]{:S(2)}) collective-permute-start(f32[128,1024]{1,0:T(8,128)S(1)} %get-tuple-element.36.chip1), channel_id=1, source_target_pairs={{8,16},{16,8},{24,32},{32,24},{40,48},{48,40},{56,64},{64,56},{72,... | collective-permute-start | bytes 1572872 | tf_op jit(solution)/shard_map/ppermute | solution.py:374
  52.7 1.9 %collective-permute-start.5 = (f32[128,1024]{1,0:T(8,128)S(1)}, f32[128,1024]{1,0:T(8,128)S(1)}, u32[]{:S(2)}, u32[]{:S(2)}) collective-permute-start(f32[128,1024]{1,0:T(8,128)S(1)} %get-tuple-element.37.core1), channel_id=1, source_target_pairs={{0,8},{8,0},{16,24},{24,16},{32,40},{40,32},{48,56},{56,48},{64,72... | collective-permute-start | bytes 1572872 | tf_op jit(solution)/shard_map/ppermute | solution.py:377
  54.6 0.0 collective-permute-done.7
  54.6 4.5 %collective-permute-start.10 = (f32[32,2816]{1,0:T(8,128)S(1)}, f32[32,2816]{1,0:T(8,128)S(1)}, u32[]{:S(2)}, u32[]{:S(2)}) collective-permute-start(f32[32,2816]{1,0:T(8,128)S(1)} %pad_maximum_fusion.rest_4_.own), channel_id=1, source_target_pairs={{0,2},{1,3},{2,0},{3,1},{4,6},{5,7},{6,4},{7,5},{8,10},{9,11},{10,... | collective-permute-start | bytes 1081352 | tf_op jit(solution)/shard_map/ppermute | solution.py:342
  59.1 2.2 %collective-permute-start.8 = (f32[32,2816]{1,0:T(8,128)S(1)}, f32[32,2816]{1,0:T(8,128)S(1)}, u32[]{:S(2)}, u32[]{:S(2)}) collective-permute-start(f32[32,2816]{1,0:T(8,128)S(1)} %pad_maximum_fusion.rest_4_.own), channel_id=1, source_target_pairs={{0,1},{1,0},{2,3},{3,2},{4,5},{5,4},{6,7},{7,6},{8,9},{9,8},{10,11... | collective-permute-start | bytes 1081352 | tf_op jit(solution)/shard_map/ppermute | solution.py:342
  61.4 2.5 %collective-permute-start.9 = (f32[32,2816]{1,0:T(8,128)S(1)}, f32[32,2816]{1,0:T(8,128)S(1)}, u32[]{:S(2)}, u32[]{:S(2)}) collective-permute-start(f32[32,2816]{1,0:T(8,128)S(1)} %pad_maximum_fusion.rest_4_.own), channel_id=1, source_target_pairs={{0,3},{1,2},{2,1},{3,0},{4,7},{5,6},{6,5},{7,4},{8,11},{9,10},{10,... | collective-permute-start | bytes 1081352 | tf_op jit(solution)/shard_map/ppermute | solution.py:342
  63.8 1.8 %shard_map.39 = (f32[512,1024]{1,0:T(8,128)S(1)}, f32[128,128]{1,0:T(8,128)S(1)}) custom-call(f32[32,2048]{1,0:T(8,128)S(1)} %pad_maximum_fusion.1.own.rest_0_, f32[32,2048]{1,0:T(8,128)S(1)} %collective-permute-done.1.left.rest_1_, f32[32,2048]{1,0:T(8,128)S(1)} %collective-permute-done.2.right.rest_2_, ...), custom_call_target="tpu_custom_call" | custom-call | flops 1207959552 | bytes 4194304 | tf_op jit(solution)/shard_map/pallas_call | solution.py:325
  65.6 1.9 %collective-permute-done.10.rest_7_.across = f32[32,2816]{1,0:T(8,128)S(1)} collective-permute-done((f32[32,2816]{1,0:T(8,128)S(1)}, f32[32,2816]{1,0:T(8,128)S(1)}, u32[]{:S(2)}, u32[]{:S(2)}) %collective-permute-start.10) | collective-permute-done | bytes 360480 | tf_op jit(solution)/shard_map/ppermute | solution.py:342
  67.5 7.7 %collective-permute-done.8.rest_5_.left = f32[32,2816]{1,0:T(8,128)S(1)} collective-permute-done((f32[32,2816]{1,0:T(8,128)S(1)}, f32[32,2816]{1,0:T(8,128)S(1)}, u32[]{:S(2)}, u32[]{:S(2)}) %collective-permute-start.8) | collective-permute-done | bytes 360480 | tf_op jit(solution)/shard_map/ppermute | solution.py:342
  75.2 0.4 collective-permute-done.9.rest_6_.right
  75.6 2.0 %shard_map.42 = (bf16[2,256,256]{2,1,0:T(8,128)(2,1)S(1)}, bf16[2,256,256]{2,1,0:T(8,128)(2,1)S(1)}, bf16[2,128,128]{2,1,0:T(8,128)(2,1)S(1)}, bf16[2,128,128]{2...) custom-call(f32[2,128,128]{2,1,0:T(8,128)S(1)} %get-tuple-element.38.nxt_t.prev, ...), custom_call_target="tpu_custom_call" | custom-call | flops 402653184 | bytes 4194304 | tf_op jit(solution)/shard_map/pallas_call | solution.py:325
  77.6 0.0 collective-permute-done.4.got1
  77.6 0.0 collective-permute-done.5.got_core1
  77.6 3.9 %shard_map.43 = (f32[512,1024]{1,0:T(8,128)S(1)}, bf16[2,256,256]{2,1,0:T(8,128)(2,1)S(1)}, bf16[2,256,256]{2,1,0:T(8,128)(2,1)S(1)}, bf16[2,128,128]{2,1,0:T(8,...) custom-call(f32[128,1024]{1,0:T(8,128)S(1)} %get-tuple-element.36.ch, ...), custom_call_target="tpu_custom_call" | custom-call | flops 2013265920 | bytes 4194304 | tf_op jit(solution)/shard_map/pallas_call | solution.py:325
  81.6 2.9 %collective-permute-start.12 = (f32[304,1024]{1,0:T(8,128)S(1)}, f32[304,1024]{1,0:T(8,128)S(1)}, u32[]{:S(2)}, u32[]{:S(2)}) collective-permute-start(f32[304,1024]{1,0:T(8,128)S(1)} %get-tuple-element.50.core35), channel_id=1, source_target_pairs={{0,8},{8,0},{16,24},{24,16},{32,40},{40,32},{48,56},{56,48},{64,72... | collective-permute-start | bytes 3735560 | tf_op jit(solution)/shard_map/ppermute | solution.py:377
  84.5 1.9 %collective-permute-start.13 = (f32[160,1024]{1,0:T(8,128)S(1)}, f32[160,1024]{1,0:T(8,128)S(1)}, u32[]{:S(2)}, u32[]{:S(2)}) collective-permute-start(f32[160,1024]{1,0:T(8,128)S(1)} %get-tuple-element.51.chip3), channel_id=1, source_target_pairs={{8,16},{16,8},{24,32},{32,24},{40,48},{48,40},{56,64},{64,56},{72,... | collective-permute-start | bytes 1966088 | tf_op jit(solution)/shard_map/ppermute | solution.py:374
  86.4 5.0 %collective-permute-start.11 = (f32[144,1024]{1,0:T(8,128)S(1)}, f32[144,1024]{1,0:T(8,128)S(1)}, u32[]{:S(2)}, u32[]{:S(2)}) collective-permute-start(f32[144,1024]{1,0:T(8,128)S(1)} %get-tuple-element.49.chip5), channel_id=1, source_target_pairs={{8,16},{16,8},{24,32},{32,24},{40,48},{48,40},{56,64},{64,56},{72,... | collective-permute-start | bytes 1769480 | tf_op jit(solution)/shard_map/ppermute | solution.py:374
  91.5 0.5 shard_map.44
  92.0 5.6 %collective-permute-done.13.got3 = f32[160,1024]{1,0:T(8,128)S(1)} collective-permute-done((f32[160,1024]{1,0:T(8,128)S(1)}, f32[160,1024]{1,0:T(8,128)S(1)}, u32[]{:S(2)}, u32[]{:S(2)}) %collective-permute-start.13) | collective-permute-done | bytes 655392 | tf_op jit(solution)/shard_map/ppermute | solution.py:374
  97.6 0.0 collective-permute-done.12.got_core35
  97.6 2.5 %shard_map.45 = (f32[2,128,1024]{2,1,0:T(8,128)S(1)}, f32[256,1024]{1,0:T(8,128)S(1)}, f32[2,128,1024]{2,1,0:T(8,128)S(1)}, bf16[2,128,128]{2,1,0:T(8,128)(2,1)S(1)}, bf16[2,128,128]{2,1,0:T(8,128)(2,1)S(1)}) custom-call(f32[128,1024]{1,0:T(8,128)S(1)} %get-tuple-element.36.chip1, f32[128,1024]{1,0:T(8,128)S(1)} %collective-permute-done.4.got1, ...), custom_call_target="tpu_custom_call" | custom-call | flops 2013265920 | bytes 4194304 | tf_op jit(solution)/shard_map/pallas_call | solution.py:325
  100.1 3.8 %collective-permute-done.11.got5 = f32[144,1024]{1,0:T(8,128)S(1)} collective-permute-done((f32[144,1024]{1,0:T(8,128)S(1)}, f32[144,1024]{1,0:T(8,128)S(1)}, u32[]{:S(2)}, u32[]{:S(2)}) %collective-permute-start.11) | collective-permute-done | bytes 589856 | tf_op jit(solution)/shard_map/ppermute | solution.py:374
  103.9 2.1 %shard_map.46 = f32[512,1024]{1,0:T(8,128)} custom-call(f32[144,1024]{1,0:T(8,128)S(1)} %get-tuple-element.49.chip5, f32[144,1024]{1,0:T(8,128)S(1)} %collective-permute-done.11.got5, f32[304,1024]{1,0:T(8,128)S(1)} %get-tuple-element.50.core35, f32[304,1024]{1,0:T(8,128)S(1)} %collective-permute-done.12.got_core35, ...), custom_call_target="tpu_custom_call" | custom-call | flops 402653184 | bytes 4194304 | tf_op jit(solution)/shard_map/pallas_call | solution.py:325
  (5 shorter events, 0.1 us)
Async XLA Ops:
  0.0 0.9 copy-start.1
  0.9 0.9 copy-start.2
  1.8 13.8 %collective-permute-start = (f32[16,2048]{1,0:T(8,128)S(1)}, f32[16,2048]{1,0:T(8,128)S(1)}, u32[]{:S(2)}, u32[]{:S(2)}) collective-permute-start(f32[16,2048]{1,0:T(8,128)S(1)} %shard_map.37), channel_id=1, source_target_pairs={{0,4},{1,5},{2,6},{3,7},{4,0},{5,1},{6,2},{7,3},{8,12},{9,13},{10,... | collective-permute-start | bytes 393224 | tf_op jit(solution)/shard_map/ppermute | solution.py:337
  15.7 27.9 %collective-permute-start.1 = (f32[32,2048]{1,0:T(8,128)S(1)}, f32[32,2048]{1,0:T(8,128)S(1)}, u32[]{:S(2)}, u32[]{:S(2)}) collective-permute-start(f32[32,2048]{1,0:T(8,128)S(1)} %pad_maximum_fusion.1.own.rest_0_), channel_id=1, source_target_pairs={{0,1},{1,0},{2,3},{3,2},{4,5},{5,4},{6,7},{7,6},{8,9},{9,8},{10,11... | collective-permute-start | bytes 786440 | tf_op jit(solution)/shard_map/ppermute | solution.py:342
  18.8 24.8 %collective-permute-start.2 = (f32[32,2048]{1,0:T(8,128)S(1)}, f32[32,2048]{1,0:T(8,128)S(1)}, u32[]{:S(2)}, u32[]{:S(2)}) collective-permute-start(f32[32,2048]{1,0:T(8,128)S(1)} %pad_maximum_fusion.1.own.rest_0_), channel_id=1, source_target_pairs={{0,3},{1,2},{2,1},{3,0},{4,7},{5,6},{6,5},{7,4},{8,11},{9,10},{10,... | collective-permute-start | bytes 786440 | tf_op jit(solution)/shard_map/ppermute | solution.py:342
  22.5 21.1 %collective-permute-start.3 = (f32[32,2048]{1,0:T(8,128)S(1)}, f32[32,2048]{1,0:T(8,128)S(1)}, u32[]{:S(2)}, u32[]{:S(2)}) collective-permute-start(f32[32,2048]{1,0:T(8,128)S(1)} %pad_maximum_fusion.1.own.rest_0_), channel_id=1, source_target_pairs={{0,2},{1,3},{2,0},{3,1},{4,6},{5,7},{6,4},{7,5},{8,10},{9,11},{10,... | collective-permute-start | bytes 786440 | tf_op jit(solution)/shard_map/ppermute | solution.py:342
  25.1 7.5 %collective-permute-start.6 = (f32[16,1024]{1,0:T(8,128)S(1)}, f32[16,1024]{1,0:T(8,128)S(1)}, u32[]{:S(2)}, u32[]{:S(2)}) collective-permute-start(f32[16,1024]{1,0:T(8,128)S(1)} %shard_map.40), channel_id=1, source_target_pairs={{0,8},{8,16},{16,24},{24,32},{32,40},{40,48},{48,56},{56,64},{64,7... | collective-permute-start | bytes 196616 | tf_op jit(solution)/shard_map/ppermute | solution.py:352
  32.6 0.9 copy-start.3
  33.6 21.0 %collective-permute-start.7 = (f32[16,2816]{1,0:T(8,128)S(1)}, f32[16,2816]{1,0:T(8,128)S(1)}, u32[]{:S(2)}, u32[]{:S(2)}) collective-permute-start(f32[16,2816]{1,0:T(8,128)S(1)} %shard_map.41), channel_id=1, source_target_pairs={{0,4},{1,5},{2,6},{3,7},{4,0},{5,1},{6,2},{7,3},{8,12},{9,13},{10,... | collective-permute-start | bytes 540680 | tf_op jit(solution)/shard_map/ppermute | solution.py:337
  43.6 1.6 %copy-start = (f32[512,1024]{1,0:T(8,128)S(1)}, f32[512,1024]{1,0:T(8,128)}, u32[]{:S(2)}) copy-start(f32[512,1024]{1,0:T(8,128)} %x.3) | copy-start | bytes 6291460
  46.9 30.7 %collective-permute-start.4 = (f32[128,1024]{1,0:T(8,128)S(1)}, f32[128,1024]{1,0:T(8,128)S(1)}, u32[]{:S(2)}, u32[]{:S(2)}) collective-permute-start(f32[128,1024]{1,0:T(8,128)S(1)} %get-tuple-element.36.chip1), channel_id=1, source_target_pairs={{8,16},{16,8},{24,32},{32,24},{40,48},{48,40},{56,64},{64,56},{72,... | collective-permute-start | bytes 1572872 | tf_op jit(solution)/shard_map/ppermute | solution.py:374
  52.7 25.0 %collective-permute-start.5 = (f32[128,1024]{1,0:T(8,128)S(1)}, f32[128,1024]{1,0:T(8,128)S(1)}, u32[]{:S(2)}, u32[]{:S(2)}) collective-permute-start(f32[128,1024]{1,0:T(8,128)S(1)} %get-tuple-element.37.core1), channel_id=1, source_target_pairs={{0,8},{8,0},{16,24},{24,16},{32,40},{40,32},{48,56},{56,48},{64,72... | collective-permute-start | bytes 1572872 | tf_op jit(solution)/shard_map/ppermute | solution.py:377
  54.6 12.9 %collective-permute-start.10 = (f32[32,2816]{1,0:T(8,128)S(1)}, f32[32,2816]{1,0:T(8,128)S(1)}, u32[]{:S(2)}, u32[]{:S(2)}) collective-permute-start(f32[32,2816]{1,0:T(8,128)S(1)} %pad_maximum_fusion.rest_4_.own), channel_id=1, source_target_pairs={{0,2},{1,3},{2,0},{3,1},{4,6},{5,7},{6,4},{7,5},{8,10},{9,11},{10,... | collective-permute-start | bytes 1081352 | tf_op jit(solution)/shard_map/ppermute | solution.py:342
  59.1 16.1 %collective-permute-start.8 = (f32[32,2816]{1,0:T(8,128)S(1)}, f32[32,2816]{1,0:T(8,128)S(1)}, u32[]{:S(2)}, u32[]{:S(2)}) collective-permute-start(f32[32,2816]{1,0:T(8,128)S(1)} %pad_maximum_fusion.rest_4_.own), channel_id=1, source_target_pairs={{0,1},{1,0},{2,3},{3,2},{4,5},{5,4},{6,7},{7,6},{8,9},{9,8},{10,11... | collective-permute-start | bytes 1081352 | tf_op jit(solution)/shard_map/ppermute | solution.py:342
  61.4 14.2 %collective-permute-start.9 = (f32[32,2816]{1,0:T(8,128)S(1)}, f32[32,2816]{1,0:T(8,128)S(1)}, u32[]{:S(2)}, u32[]{:S(2)}) collective-permute-start(f32[32,2816]{1,0:T(8,128)S(1)} %pad_maximum_fusion.rest_4_.own), channel_id=1, source_target_pairs={{0,3},{1,2},{2,1},{3,0},{4,7},{5,6},{6,5},{7,4},{8,11},{9,10},{10,... | collective-permute-start | bytes 1081352 | tf_op jit(solution)/shard_map/ppermute | solution.py:342
  81.6 16.0 %collective-permute-start.12 = (f32[304,1024]{1,0:T(8,128)S(1)}, f32[304,1024]{1,0:T(8,128)S(1)}, u32[]{:S(2)}, u32[]{:S(2)}) collective-permute-start(f32[304,1024]{1,0:T(8,128)S(1)} %get-tuple-element.50.core35), channel_id=1, source_target_pairs={{0,8},{8,0},{16,24},{24,16},{32,40},{40,32},{48,56},{56,48},{64,72... | collective-permute-start | bytes 3735560 | tf_op jit(solution)/shard_map/ppermute | solution.py:377
  84.5 13.1 %collective-permute-start.13 = (f32[160,1024]{1,0:T(8,128)S(1)}, f32[160,1024]{1,0:T(8,128)S(1)}, u32[]{:S(2)}, u32[]{:S(2)}) collective-permute-start(f32[160,1024]{1,0:T(8,128)S(1)} %get-tuple-element.51.chip3), channel_id=1, source_target_pairs={{8,16},{16,8},{24,32},{32,24},{40,48},{48,40},{56,64},{64,56},{72,... | collective-permute-start | bytes 1966088 | tf_op jit(solution)/shard_map/ppermute | solution.py:374
  86.4 17.5 %collective-permute-start.11 = (f32[144,1024]{1,0:T(8,128)S(1)}, f32[144,1024]{1,0:T(8,128)S(1)}, u32[]{:S(2)}, u32[]{:S(2)}) collective-permute-start(f32[144,1024]{1,0:T(8,128)S(1)} %get-tuple-element.49.chip5), channel_id=1, source_target_pairs={{8,16},{16,8},{24,32},{32,24},{40,48},{48,40},{56,64},{64,56},{72,... | collective-permute-start | bytes 1769480 | tf_op jit(solution)/shard_map/ppermute | solution.py:374
